TPU v7x, 128 devices: a whole 4x4x4 slice. The times are simulated.
128 devices in a mesh: dp: 1, cy: 16 (over z, y), cx: 8 (over x, core).
Axes of the slice: x: 4, y: 4, z: 4, core: 2. Of those that a mesh axis runs over, the one named last changes fastest.
Arguments:
- query_rows: bfloat16 [16384, 32, 128], P(('dp', 'cy', 'cx'))
- key_rows: bfloat16 [16384, 8, 128], P(('dp', 'cy', 'cx'))
- value_rows: bfloat16 [16384, 8, 128], P(('dp', 'cy', 'cx'))
- out_rows: bfloat16 [16384, 32, 128], P(('dp', 'cy', 'cx'))
- grad_out: bfloat16 [16384, 32, 128], P(('dp', 'cy', 'cx'))
- log_sum_exp: float32 [16384, 32], P(('dp', 'cy', 'cx'))
Outputs:
- output 1: bfloat16 [16384, 32, 128], P(('dp', 'cy', 'cx'))
- output 2: bfloat16 [16384, 8, 128], P(('dp', 'cy', 'cx'))
- output 3: bfloat16 [16384, 8, 128], P(('dp', 'cy', 'cx'))
All inputs are finite; a program needn't handle non-finite values.
Results may differ from a plain program's by a relative error of at most 0.0112.
Values are sent between devices in bfloat16 or wider.
A program may use at most 1 GiB of HBM per device.

v0:
```python
import math
import jax
import jax.numpy as jnp
from jax import lax
from jax.sharding import PartitionSpec as P


def block_grads(q_blk, do_blk, lse_blk, delta_blk, k_blk, v_blk, keep_mask, scaling):
    score_f32 = jnp.einsum('qkgd,skd->kqgs', q_blk, k_blk, preferred_element_type=jnp.float32) * scaling
    prob_f32 = jnp.exp(score_f32 - lse_blk[..., None])
    if keep_mask is not None:
        prob_f32 = jnp.where(keep_mask[None, :, None, :], prob_f32, 0.0)
    dprob_f32 = jnp.einsum('qkgd,skd->kqgs', do_blk, v_blk, preferred_element_type=jnp.float32)
    dscore_b16 = (prob_f32 * (dprob_f32 - delta_blk[..., None])).astype(jnp.bfloat16)
    prob_b16 = prob_f32.astype(jnp.bfloat16)
    dq_part = jnp.einsum('kqgs,skd->kqgd', dscore_b16, k_blk, preferred_element_type=jnp.float32)
    dk_part = jnp.einsum('kqgs,qkgd->ksd', dscore_b16, q_blk, preferred_element_type=jnp.float32)
    dv_part = jnp.einsum('kqgs,qkgd->ksd', prob_b16, do_blk, preferred_element_type=jnp.float32)
    return dq_part, dk_part, dv_part


def solution(mesh):
    n_cx = mesh.shape['cx']
    n_ctx = mesh.shape['cy'] * n_cx
    ctx_axes = ('cy', 'cx')
    shift_perm = [(dev_idx, (dev_idx + 1) % n_ctx) for dev_idx in range(n_ctx)]
    row_spec = P(('dp', 'cy', 'cx'), None, None)
    stat_spec = P(('dp', 'cy', 'cx'), None)

    def local_grads(query_rows, key_rows, value_rows, out_rows, grad_out, log_sum_exp):
        tok_dev, n_heads, head_dim = query_rows.shape
        kv_heads = key_rows.shape[1]
        group_size = n_heads // kv_heads
        half_tok = tok_dev // 2
        scaling = 1.0 / math.sqrt(head_dim)
        ctx_rank = lax.axis_index('cy') * n_cx + lax.axis_index('cx')
        q_grp = query_rows.reshape(tok_dev, kv_heads, group_size, head_dim)
        do_grp = grad_out.reshape(tok_dev, kv_heads, group_size, head_dim)
        lse_grp = log_sum_exp.reshape(tok_dev, kv_heads, group_size).transpose(1, 0, 2)
        delta_grp = jnp.einsum('thd,thd->th', grad_out, out_rows, preferred_element_type=jnp.float32).reshape(tok_dev, kv_heads, group_size).transpose(1, 0, 2)
        local_idx = jnp.arange(tok_dev)
        piece_id = jnp.where(local_idx < half_tok, ctx_rank, 2 * n_ctx - 1 - ctx_rank)
        own_pos = piece_id * half_tok + local_idx % half_tok
        diag_mask = own_pos[:, None] >= own_pos[None, :]
        dq_own, dk_own, dv_own = block_grads(q_grp, do_grp, lse_grp, delta_grp, key_rows, value_rows, diag_mask, scaling)

        def src_before(k_blk, v_blk):
            dq_part, dk_part, dv_part = block_grads(q_grp, do_grp, lse_grp, delta_grp, k_blk[:half_tok], v_blk[:half_tok], None, scaling)
            zero_pad = jnp.zeros_like(dk_part)
            return dq_part, jnp.concatenate([dk_part, zero_pad], axis=1), jnp.concatenate([dv_part, zero_pad], axis=1)

        def src_after(k_blk, v_blk):
            dq_part, dk_part, dv_part = block_grads(q_grp[half_tok:], do_grp[half_tok:], lse_grp[:, half_tok:], delta_grp[:, half_tok:], k_blk, v_blk, None, scaling)
            zero_pad = jnp.zeros_like(dq_part)
            return jnp.concatenate([zero_pad, dq_part], axis=1), dk_part, dv_part

        def step_body(step_idx, state):
            k_cur, v_cur, dk_cur, dv_cur, dq_cur = state
            k_cur = lax.ppermute(k_cur, ctx_axes, shift_perm)
            v_cur = lax.ppermute(v_cur, ctx_axes, shift_perm)
            dk_cur = lax.ppermute(dk_cur, ctx_axes, shift_perm)
            dv_cur = lax.ppermute(dv_cur, ctx_axes, shift_perm)
            src_rank = (ctx_rank - step_idx) % n_ctx
            dq_part, dk_part, dv_part = lax.cond(src_rank < ctx_rank, src_before, src_after, k_cur, v_cur)
            return (k_cur, v_cur, dk_cur + dk_part, dv_cur + dv_part, dq_cur + dq_part)

        k_end, v_end, dk_end, dv_end, dq_end = lax.fori_loop(1, n_ctx, step_body, (key_rows, value_rows, dk_own, dv_own, dq_own))
        dk_home = lax.ppermute(dk_end, ctx_axes, shift_perm)
        dv_home = lax.ppermute(dv_end, ctx_axes, shift_perm)
        grad_query = (dq_end * scaling).astype(jnp.bfloat16).transpose(1, 0, 2, 3).reshape(tok_dev, n_heads, head_dim)
        grad_key = (dk_home * scaling).astype(jnp.bfloat16).transpose(1, 0, 2)
        grad_value = dv_home.astype(jnp.bfloat16).transpose(1, 0, 2)
        return grad_query, grad_key, grad_value

    return jax.shard_map(local_grads, mesh=mesh, in_specs=(row_spec, row_spec, row_spec, row_spec, row_spec, stat_spec), out_specs=(row_spec, row_spec, row_spec), check_vma=False)
```

profile of v0, /device:TPU:1, one launch (start us, length us, event | category | flops | bytes accessed | tf_op | source)
XLA Modules:
  0.0 5099.0 jit_solution(3120785732801657589)
XLA Ops:
  11.2 5060.0 %while.23 = (s32[]{:T(128)}, bf16[128,8,128]{2,0,1:T(8,128)(2,1)}, bf16[128,8,128]{2,0,1:T(8,128)(2,1)}, f32[8,128,128]{2,1,0:T(8,128)}, f32[8,128,128]{2,1,0:T(...) while((s32[]{:T(128)}, bf16[128,8,128]{2,0,1:T(8,128)(2,1)}, ...), condition=%wide.region_3.4_spmd, body=%wide.region_0.3_spmd.sunk | while | flops 337903616 | bytes 30310964 | solution.py:67
  231.4 24.8 collective-permute-done
  271.4 24.8 collective-permute-done
  351.4 24.8 collective-permute-done
  391.4 24.8 collective-permute-done
  471.4 24.8 collective-permute-done
  511.4 24.8 collective-permute-done
  591.4 24.8 collective-permute-done
  631.4 24.8 collective-permute-done
  711.4 24.8 collective-permute-done
  751.4 24.8 collective-permute-done
  831.4 24.8 collective-permute-done
  871.4 24.8 collective-permute-done
  951.4 24.8 collective-permute-done
  991.4 24.8 collective-permute-done
  1071.4 24.8 collective-permute-done
  1111.4 24.8 collective-permute-done
  1191.4 24.8 collective-permute-done
  1231.4 24.8 collective-permute-done
  1311.4 24.8 collective-permute-done
  1351.4 24.8 collective-permute-done
  1431.4 24.8 collective-permute-done
  1471.4 24.8 collective-permute-done
  1551.4 24.8 collective-permute-done
  1591.4 24.8 collective-permute-done
  1671.4 24.8 collective-permute-done
  1711.4 24.8 collective-permute-done
  1791.4 24.8 collective-permute-done
  1831.4 24.8 collective-permute-done
  1911.4 24.8 collective-permute-done
  1951.4 24.8 collective-permute-done
  2031.4 24.8 collective-permute-done
  2071.4 24.8 collective-permute-done
  2151.4 24.8 collective-permute-done
  2191.4 24.8 collective-permute-done
  2271.4 24.8 collective-permute-done
  2311.4 24.8 collective-permute-done
  2391.4 24.8 collective-permute-done
  2431.4 24.8 collective-permute-done
  2511.4 24.8 collective-permute-done
  2551.4 24.8 collective-permute-done
  2631.4 24.8 collective-permute-done
  2671.4 24.8 collective-permute-done
  2751.4 24.8 collective-permute-done
  2791.4 24.8 collective-permute-done
  2871.4 24.8 collective-permute-done
  2991.4 24.8 collective-permute-done
  3111.4 24.8 collective-permute-done
  3231.4 24.8 collective-permute-done
  3351.4 24.8 collective-permute-done
  3471.4 24.8 collective-permute-done
  3591.4 24.8 collective-permute-done
  3711.4 24.8 collective-permute-done
  3831.4 24.8 collective-permute-done
  3951.4 24.8 collective-permute-done
  4071.4 24.8 collective-permute-done
  4191.4 24.8 collective-permute-done
  4311.4 24.8 collective-permute-done
  4431.4 24.8 collective-permute-done
  4551.4 24.8 collective-permute-done
  4671.4 24.8 collective-permute-done
  4791.4 24.8 collective-permute-done
  4911.4 24.8 collective-permute-done
  5031.4 24.8 collective-permute-done
  (2763 shorter events, 4110.4 us)
Async XLA Ops:
  231.3 38.1 collective-permute-start.2
  271.3 38.1 collective-permute-start.2
  351.3 38.1 collective-permute-start.2
  391.3 38.1 collective-permute-start.2
  471.3 38.1 collective-permute-start.2
  511.3 38.1 collective-permute-start.2
  591.3 38.1 collective-permute-start.2
  631.3 38.1 collective-permute-start.2
  711.3 38.1 collective-permute-start.2
  751.3 38.1 collective-permute-start.2
  831.3 38.1 collective-permute-start.2
  871.3 38.1 collective-permute-start.2
  951.3 38.1 collective-permute-start.2
  991.3 38.1 collective-permute-start.2
  1071.3 38.1 collective-permute-start.2
  1111.3 38.1 collective-permute-start.2
  1191.3 38.1 collective-permute-start.2
  1231.3 38.1 collective-permute-start.2
  1311.3 38.1 collective-permute-start.2
  1351.3 38.1 collective-permute-start.2
  1431.3 38.1 collective-permute-start.2
  1471.3 38.1 collective-permute-start.2
  1551.3 38.1 collective-permute-start.2
  1591.3 38.1 collective-permute-start.2
  1671.3 38.1 collective-permute-start.2
  1711.3 38.1 collective-permute-start.2
  1791.3 38.1 collective-permute-start.2
  1831.3 38.1 collective-permute-start.2
  1911.3 38.1 collective-permute-start.2
  1951.3 38.1 collective-permute-start.2
  2031.3 38.1 collective-permute-start.2
  2071.3 38.1 collective-permute-start.2
  2151.3 38.1 collective-permute-start.2
  2191.3 38.1 collective-permute-start.2
  2271.3 38.1 collective-permute-start.2
  2311.3 38.1 collective-permute-start.2
  2391.3 38.1 collective-permute-start.2
  2431.3 38.1 collective-permute-start.2
  2511.3 38.1 collective-permute-start.2
  2551.3 38.1 collective-permute-start.2
  2631.3 38.1 collective-permute-start.2
  2671.3 38.1 collective-permute-start.2
  2751.3 38.1 collective-permute-start.2
  2791.3 38.1 collective-permute-start.2
  2871.3 38.1 collective-permute-start.2
  2911.3 38.1 collective-permute-start.2
  2991.3 38.1 collective-permute-start.2
  3111.3 38.1 collective-permute-start.2
  3231.3 38.1 collective-permute-start.2
  3351.3 38.1 collective-permute-start.2
  3471.3 38.1 collective-permute-start.2
  3591.3 38.1 collective-permute-start.2
  3711.3 38.1 collective-permute-start.2
  3831.3 38.1 collective-permute-start.2
  3951.3 38.1 collective-permute-start.2
  4071.3 38.1 collective-permute-start.2
  4191.3 38.1 collective-permute-start.2
  4311.3 38.1 collective-permute-start.2
  4431.3 38.1 collective-permute-start.2
  4551.3 38.1 collective-permute-start.2
  4671.3 38.1 collective-permute-start.2
  4791.3 38.1 collective-permute-start.2
  4911.3 38.1 collective-permute-start.2
  5031.3 38.1 collective-permute-start.2
  (451 other events, 13297.1 us)
where the time goes:
time: 5130 us; the launch traced here: 5100 us
  waiting for transfers between devices  3180 us (62%)
  other arithmetic  984 us (19%)
  local copies, waits for them, and re-layouts  525 us (10%)
  matrix products  373 us (7%)
    ppermute x127, waiting for transfers between devices, step_body(): k_cur = lax.ppermute(k_cur, ctx_axes, shift_perm)  3110 us
    add x381, other arithmetic, step_body(): return (k_cur, v_cur, dk_cur + dk_part, dv_cur + dv_part, dq_cur + dq_part)  981 us
    while x254, local copies, waits for them, and re-layouts  301 us
    concatenate x126, local copies, waits for them, and re-layouts, src_after(): return (jnp.concatenate([zero_pad, dq_part], axis=1), dk_part, dv_part)  196 us
    dot_general x128, matrix products, block_grads(): jnp.einsum('qkgd,skd->kqgs', do_blk, v_blk, preferred_element_type=jnp.fl...  170 us
  transfers between devices with their start and end apart: 510, of which 255 were waited for; matrix products, arithmetic and copies ran while one was open for 32% of the time, Pallas kernels for 0%

commit v1 on v0

v1 whole, which is shorter than its diff:
```python
import math
import jax
import jax.numpy as jnp
from jax import lax
from jax.experimental import pallas as pl
from jax.experimental.pallas import tpu as pltpu
from jax.sharding import PartitionSpec as P

f32, bf16 = jnp.float32, jnp.bfloat16
LOG2E = 1.4426950408889634
SCALE = 1.0 / math.sqrt(128.0)
NT = (((1,), (1,)), ((), ()))
TN = (((0,), (0,)), ((), ()))
MESH = pl.DeviceIdType.MESH


def _step_j(k):
    odd = k % 2
    return odd * ((k + 1) // 2) + (1 - odd) * (8 - k // 2)


def _kernel(qd_in, st_in, kv_in, out_dq, out_dkv,
            qd, stb, st2, kv, dq, acc, rx, dqx, dqs, dks,
            loc_s, qd_s, qd_r, st_s, st_r, kvo_s, kvo_r, kvg_s, kvg_r, fw_s, fw_r,
            rs_s, rs_r, dqx_s, dqx_r, odq_s, odq_r, odk_s, odk_r):
    cy, cx = lax.axis_index("cy"), lax.axis_index("cx")
    rem, div = lax.rem, lax.div
    x, c = div(cx, 2), rem(cx, 2)
    yl, s = rem(cy, 2), div(cy, 2)
    bs = rem(s, 2)
    a = rem(yl + bs, 2)
    i = yl * 4 + x
    h = a * 4 + x

    def member(i2):
        yl2, x2 = div(i2, 4), rem(i2, 4)
        return {"cy": 2 * s + yl2, "cx": 2 * x2 + c}, rem(yl2 + bs, 2) * 4 + x2

    def peer(s2):
        return {"cy": 2 * s2 + rem(a + rem(s2, 2), 2), "cx": cx}

    partner = {"cy": cy, "cx": cx + 1 - 2 * c}

    def slot(el, i2):
        return i2 + el * (7 - 2 * i2)

    def rows(cp, el, i2):
        return pl.ds(pl.multiple_of(cp * 1024 + el * 512 + slot(el, i2) * 64, 64), 64)

    def remote(src, dst, ssem, rsem, dev):
        return pltpu.make_async_remote_copy(src, dst, ssem, rsem, device_id=dev, device_id_type=MESH)

    def arrived(ref, ssem, rsem):
        remote(ref, ref, ssem, rsem, partner).wait_recv()

    loc = [pltpu.make_async_copy(kv_in.at[h, 0], kv.at[s, 0, :, pl.ds(pl.multiple_of(i * 64, 64), 64), :], loc_s.at[0]),
           pltpu.make_async_copy(kv_in.at[h, 1], kv.at[s, 1, :, pl.ds(pl.multiple_of((7 - i) * 64, 64), 64), :], loc_s.at[1]),
           pltpu.make_async_copy(st_in.at[h], stb.at[c, i], loc_s.at[2]),
           pltpu.make_async_copy(qd_in.at[h, 1], qd.at[:, :, rows(c, 1, i), :], loc_s.at[3]),
           pltpu.make_async_copy(qd_in.at[h, 0], qd.at[:, :, rows(c, 0, i), :], loc_s.at[4])]
    for cp_ in loc:
        cp_.start()

    bar = pltpu.get_barrier_semaphore()
    pl.semaphore_signal(bar, inc=1, device_id=partner, device_id_type=MESH)
    for t in range(1, 8):
        pl.semaphore_signal(bar, inc=1, device_id=member(rem(i + t, 8))[0], device_id_type=MESH)
        pl.semaphore_signal(bar, inc=1, device_id=peer(rem(s + t, 8)), device_id_type=MESH)
    pl.semaphore_wait(bar, 15)

    sends = []

    def go(cp_):
        cp_.start()
        sends.append(cp_)

    others = [member(rem(i + t, 8)) for t in range(1, 8)]
    for t, (dev, h2) in enumerate(others):
        go(remote(kv_in.at[h2, 0], kv.at[s, 0, :, pl.ds(pl.multiple_of(i * 64, 64), 64), :], kvo_s.at[0, t], kvo_r.at[0, i], dev))
        go(remote(kv_in.at[h2, 1], kv.at[s, 1, :, pl.ds(pl.multiple_of((7 - i) * 64, 64), 64), :], kvo_s.at[1, t], kvo_r.at[1, i], dev))
        go(remote(st_in.at[h2], stb.at[c, i], st_s.at[t], st_r.at[i], dev))
    for el in (1, 0):
        for t, (dev, h2) in enumerate(others):
            go(remote(qd_in.at[h2, el], qd.at[:, :, rows(c, el, i), :], qd_s.at[el, t], qd_r.at[el, i], dev))

    def zero_acc(n, carry):
        acc[n] = jnp.zeros(acc.shape[1:], f32)
        return carry

    lax.fori_loop(0, 8, zero_acc, 0)
    for hh in range(4):
        dq[hh] = jnp.zeros(dq.shape[1:], f32)

    for el in (0, 1):
        loc[el].wait()
        for t in range(1, 8):
            i2 = rem(i + t, 8)
            arrived(kv.at[s, el, :, pl.ds(pl.multiple_of(slot(el, i2) * 64, 64), 64), :], kvo_s.at[el, t - 1], kvo_r.at[el, i2])
    for k in range(1, 8):
        s2 = rem(s + _step_j(k), 8)
        go(remote(kv.at[s, 0], kv.at[s, 0], kvg_s.at[0, k], kvg_r.at[0, s], peer(s2)))

        @pl.when(s > s2)
        def _():
            remote(kv.at[s, 1], kv.at[s, 1], kvg_s.at[1, k], kvg_r.at[1, s], peer(s2)).start()

    def build_stats(cp):
        for i2 in range(8):
            tile = jnp.transpose(stb[cp, i2])
            st2[rows(cp, 0, i2), :] = tile[:64]
            st2[rows(cp, 1, i2), :] = tile[64:]

    def half(cp, el):
        return qd.at[:, :, pl.ds(pl.multiple_of(cp * 1024 + el * 512, 512), 512), :]

    def forward(el):
        return remote(half(c, el), half(c, el), fw_s.at[el], fw_r.at[el], partner)

    loc[2].wait()
    for t in range(1, 8):
        i2 = rem(i + t, 8)
        arrived(stb.at[c, i2], st_s.at[t - 1], st_r.at[i2])
    st_fw = remote(stb.at[c], stb.at[c], fw_s.at[2], fw_r.at[2], partner)
    go(st_fw)
    build_stats(c)
    loc[3].wait()
    for t in range(1, 8):
        i2 = rem(i + t, 8)
        arrived(qd.at[:, :, rows(c, 1, i2), :], qd_s.at[1, t - 1], qd_r.at[1, i2])
    go(forward(1))

    def tiles(r0, kref, vref, dkref, dvref, pq=None, pk=None):
        def s1(hh, u):
            nk = 256 if (pq is not None and u == 0) else 512
            r = pl.ds(r0 + 256 * u, 256)
            l2 = st2[r, hh:hh + 1]
            d = st2[r, 4 + hh:5 + hh]
            sc = lax.dot_general(qd[0, hh, r, :], kref[0:nk, :], NT, preferred_element_type=f32)
            dp = lax.dot_general(qd[1, hh, r, :], vref[0:nk, :], NT, preferred_element_type=f32)
            p = jnp.exp2(sc * (SCALE * LOG2E) - l2)
            if pq is not None:
                rr = lax.broadcasted_iota(jnp.int32, (256, nk), 0) + 256 * u
                kk = lax.broadcasted_iota(jnp.int32, (256, nk), 1)
                qpos = (rr >> 6) * 128 + (rr & 63) + pq * 64
                kpos = (kk >> 6) * 128 + (kk & 63) + pk * 64
                p = jnp.where(qpos >= kpos, p, 0.0)
            return p.astype(bf16), (p * (dp - d)).astype(bf16)

        todo = [(hh, u) for u in range(2) for hh in range(4)]
        now = s1(*todo[0])
        for n, (hh, u) in enumerate(todo):
            nxt = s1(*todo[n + 1]) if n + 1 < len(todo) else None
            pb, ds = now
            nk = pb.shape[1]
            r = pl.ds(r0 + 256 * u, 256)
            dkref[:, 0:nk] += lax.dot_general(qd[0, hh, r, :], ds, TN, preferred_element_type=f32)
            dvref[:, 0:nk] += lax.dot_general(qd[1, hh, r, :], pb, TN, preferred_element_type=f32)
            dq[hh, r, :] += jnp.dot(ds, kref[0:nk, :], preferred_element_type=f32)
            now = nxt

    def send_acc(k, g, kel):
        remote(acc.at[k, kel], rx.at[s, kel], rs_s.at[kel, k], rs_r.at[kel, s], peer(g)).start()

    def full_unit(n, carry):
        k, u = div(n + 2, 4), rem(n + 2, 4)
        live = div(k + 7, 8)
        sub = div(u, 2) * live
        g = rem(s + 8 - _step_j(k) * live, 8)
        gt = div(g - s + 7, 8)
        el = 1 - sub + sub * gt
        kel = sub * gt
        cp = rem(c + u, 2)

        @pl.when(n == 1)
        def _():
            arrived(stb.at[1 - c], fw_s.at[2], fw_r.at[2])
            build_stats(1 - c)
            arrived(half(1 - c, 1), fw_s.at[1], fw_r.at[1])

        @pl.when(n == 2)
        def _():
            loc[4].wait()
            for t in range(1, 8):
                i2 = rem(i + t, 8)
                arrived(qd.at[:, :, rows(c, 0, i2), :], qd_s.at[0, t - 1], qd_r.at[0, i2])
            forward(0).start()

        @pl.when(n == 4)
        def _():
            arrived(half(1 - c, 0), fw_s.at[0], fw_r.at[0])

        @pl.when((n >= 2) & (u == 0))
        def _():
            arrived(kv.at[g, 0], kvg_s.at[0, k], kvg_r.at[0, g])

        @pl.when((n >= 2) & (u == 2) & (gt == 1))
        def _():
            arrived(kv.at[g, 1], kvg_s.at[1, k], kvg_r.at[1, g])

        r0 = pl.multiple_of(cp * 1024 + el * 512, 512)
        tiles(r0, kv.at[g, kel, 0], kv.at[g, kel, 1], acc.at[k, kel, 0], acc.at[k, kel, 1])

        @pl.when((n >= 2) & (((u == 1) & (gt == 1)) | ((u == 3) & (gt == 0))))
        def _():
            send_acc(k, g, 0)

        @pl.when((n >= 2) & (u == 3) & (gt == 1))
        def _():
            send_acc(k, g, 1)

        return carry

    lax.fori_loop(0, 30, full_unit, 0)

    def dqx_copy(el):
        src = dq.at[:, pl.ds(pl.multiple_of((1 - c) * 1024 + el * 512, 512), 512), :]
        return remote(src, dqx.at[el], dqx_s.at[el], dqx_r.at[el], partner)

    def finish_dq(el):
        arrived(dqx.at[el], dqx_s.at[el], dqx_r.at[el])
        mine = pl.ds(pl.multiple_of(c * 1024 + el * 512, 512), 512)
        for hh in range(4):
            dqs[el, hh] = ((dq[hh, mine, :] + dqx[el, hh]) * SCALE).astype(bf16)

        def block(i2):
            return dqs.at[el, :, pl.ds(pl.multiple_of(slot(el, i2) * 64, 64), 64), :]

        for t in range(1, 8):
            i2 = rem(i + t, 8)
            remote(block(i2), out_dq.at[h, el], odq_s.at[el, t], odq_r.at[el, h], member(i2)[0]).start()
        pltpu.make_async_copy(block(i), out_dq.at[h, el], odq_s.at[el, 0]).start()

    def diag_unit(m, carry):
        el = div(m, 2)
        cp = rem(c + 1 + m, 2)
        r0 = pl.multiple_of(cp * 1024 + el * 512, 512)
        tiles(r0, kv.at[s, el, 0], kv.at[s, el, 1], acc.at[0, el, 0], acc.at[0, el, 1],
              pq=rem(cp + el, 2), pk=rem(c + el, 2))

        @pl.when(rem(m, 2) == 0)
        def _():
            dqx_copy(el).start()

        @pl.when(rem(m, 2) == 1)
        def _():
            finish_dq(el)

        return carry

    lax.fori_loop(0, 4, diag_unit, 0)

    for el in (0, 1):
        for k in range(1, 8):
            s3 = rem(s + _step_j(k), 8)

            def take():
                arrived(rx.at[s3, el], rs_s.at[el, k], rs_r.at[el, s3])
                acc[0, el] += rx[s3, el]

            if el == 0:
                take()
            else:
                pl.when(s > s3)(take)
        dks[el, 0] = (jnp.transpose(acc[0, el, 0]) * SCALE).astype(bf16)
        dks[el, 1] = jnp.transpose(acc[0, el, 1]).astype(bf16)

        def kblock(i2):
            return dks.at[el, :, pl.ds(pl.multiple_of(slot(el, i2) * 64, 64), 64), :]

        for t in range(1, 8):
            i2 = rem(i + t, 8)
            remote(kblock(i2), out_dkv.at[h, el], odk_s.at[el, t], odk_r.at[el, h], member(i2)[0]).start()
        pltpu.make_async_copy(kblock(i), out_dkv.at[h, el], odk_s.at[el, 0]).start()

    for cp_ in sends:
        cp_.wait_send()
    forward(0).wait_send()
    for k in range(1, 8):
        s2 = rem(s + _step_j(k), 8)

        @pl.when(s > s2)
        def _():
            remote(kv.at[s, 1], kv.at[s, 1], kvg_s.at[1, k], kvg_r.at[1, s], peer(s2)).wait_send()

        g = rem(s + 8 - _step_j(k), 8)
        remote(acc.at[k, 0], rx.at[s, 0], rs_s.at[0, k], rs_r.at[0, s], peer(g)).wait_send()

        @pl.when(g > s)
        def _():
            remote(acc.at[k, 1], rx.at[s, 1], rs_s.at[1, k], rs_r.at[1, s], peer(g)).wait_send()
    for el in (0, 1):
        dqx_copy(el).wait_send()
        pltpu.make_async_copy(dqs.at[el, :, pl.ds(0, 64), :], out_dq.at[h, el], odq_s.at[el, 0]).wait()
        pltpu.make_async_copy(dks.at[el, :, pl.ds(0, 64), :], out_dkv.at[h, el], odk_s.at[el, 0]).wait()
        for t in range(1, 8):
            dev, h2 = member(rem(i + t, 8))
            remote(dqs.at[el, :, pl.ds(0, 64), :], out_dq.at[h, el], odq_s.at[el, t], odq_r.at[el, h], dev).wait_send()
            remote(dks.at[el, :, pl.ds(0, 64), :], out_dkv.at[h, el], odk_s.at[el, t], odk_r.at[el, h], dev).wait_send()
            arrived(out_dq.at[h2, el], odq_s.at[el, t], odq_r.at[el, h2])
            arrived(out_dkv.at[h2, el], odk_s.at[el, t], odk_r.at[el, h2])


def solution(mesh):
    row_spec = P(('dp', 'cy', 'cx'), None, None)
    stat_spec = P(('dp', 'cy', 'cx'), None)

    def local(q, k, v, o, do, lse):
        T, H, D = q.shape
        G = k.shape[1]
        R = H // G
        half = T // 2
        delta = jnp.sum(do.astype(f32) * o.astype(f32), axis=-1)
        st_in = jnp.stack([lse * LOG2E, delta]).reshape(2, T, G, R).transpose(2, 0, 3, 1).reshape(G, 2 * R, T)
        qd_in = jnp.stack([q, do]).reshape(2, 2, half, G, R, D).transpose(3, 1, 0, 4, 2, 5)
        kv_in = jnp.stack([k, v]).reshape(2, 2, half, G, D).transpose(3, 1, 0, 2, 4)
        hbm = pl.BlockSpec(memory_space=pl.ANY)
        V, S = pltpu.VMEM, pltpu.SemaphoreType.DMA
        dq_o, dkv_o = pl.pallas_call(
            _kernel,
            in_specs=[hbm] * 3,
            out_specs=[hbm] * 2,
            out_shape=[jax.ShapeDtypeStruct((G, 2, R, half, D), bf16), jax.ShapeDtypeStruct((G, 2, 2, half, D), bf16)],
            scratch_shapes=[
                V((2, R, 2048, D), bf16), V((2, 8, 8, T), f32), V((2048, 8), f32), V((8, 2, 2, 512, D), bf16),
                V((R, 2048, D), f32), V((8, 2, 2, D, 512), f32), V((8, 2, 2, D, 512), f32), V((2, R, 512, D), f32),
                V((2, R, 512, D), bf16), V((2, 2, 512, D), bf16),
                S((5,)), S((2, 7)), S((2, 8)), S((7,)), S((8,)), S((2, 7)), S((2, 8)), S((2, 8)), S((2, 8)), S((3,)), S((3,)),
                S((2, 8)), S((2, 8)), S((2,)), S((2,)), S((2, 8)), S((2, 8)), S((2, 8)), S((2, 8)),
            ],
            compiler_params=pltpu.CompilerParams(collective_id=0, has_side_effects=True, vmem_limit_bytes=60 << 20),
            cost_estimate=pl.CostEstimate(flops=46 << 30, bytes_accessed=8 << 20, transcendentals=36 << 20),
            name="attn_bwd",
        )(qd_in, st_in, kv_in)
        grad_q = dq_o.transpose(1, 3, 0, 2, 4).reshape(T, H, D)
        grad_kv = dkv_o.transpose(2, 1, 3, 0, 4).reshape(2, T, G, D)
        return grad_q, grad_kv[0], grad_kv[1]

    return jax.shard_map(local, mesh=mesh, in_specs=(row_spec,) * 5 + (stat_spec,), out_specs=(row_spec,) * 3, check_vma=False)
```

time: 5130 us -> 187 us (0.04)
  the two profiles are of different devices: /device:TPU:1 before, /device:TPU:80 now
where the time goes in v1:
time: 187 us; the launch traced here: 186 us
  Pallas kernels  175 us (94%)
  local copies, waits for them, and re-layouts  8.02 us (4%)
  other arithmetic  3.03 us (2%)
    pallas_call x1, Pallas kernels, local(): pl.pallas_call(_kernel, in_specs=[hbm] * 3, out_specs=[hbm] * 2, out_shap...  175 us
    unnamed x17, local copies, waits for them, and re-layouts  3.97 us

profile of v1, /device:TPU:80, one launch (start us, length us, event | category | flops | bytes accessed | tf_op | source)
XLA Modules:
  0.0 186.4 jit_solution(16206455765008157712)
XLA Ops:
  0.6 0.0 copy-start
  0.6 1.7 copy.39
  2.4 0.0 copy-done
  2.4 0.4 copy.40
  2.8 0.0 copy-start.3
  2.8 0.0 copy-start.4
  2.8 1.5 maximum_bitcast_fusion.qd_in
  4.3 0.0 copy-done.3
  4.3 0.0 copy-start.1
  4.3 0.0 copy-start.5
  4.4 0.0 copy-done.4
  4.4 0.8 maximum_bitcast_fusion.1.kv_in
  5.3 0.5 copy-done.1
  5.8 0.6 multiply_reduce_fusion
  6.4 0.1 copy.41
  6.5 0.0 copy-done.5
  6.5 0.6 copy.42
  7.1 174.6 %attn_bwd.1 = (bf16[8,2,4,64,128]{4,3,2,1,0:T(8,128)(2,1)}, bf16[8,2,2,64,128]{4,3,2,1,0:T(8,128)(2,1)}) custom-call(bf16[8,2,2,4,64,128]{5,4,3,2,1,0:T(8,128)(2,1)} %maximum_bitcast_fusion.qd_in, f32[8,8,128]{2,1,0:T(8,128)} %bitcast.29, bf16[8,2,2,64,128]{4,3,2,1,0:T(8,128)(2,1)} %maximum_bitcast_fusion.1.kv_in), custom_call_target="tpu_custom_call" | custom-call | flops 49392123904 | bytes 8388608 | tf_op jit(solution)/shard_map/attn_bwd/pallas_call | solution.py:318
  181.8 0.0 copy-start.2
  181.8 1.2 fusion
  182.9 0.9 copy.47
  183.8 0.9 copy.48
  184.7 0.0 copy-done.2
  184.7 0.1 copy.45
  184.8 1.6 copy.46
  (4 shorter events, 0.1 us)
Async XLA Ops:
  0.6 1.7 copy-start
  2.8 1.6 copy-start.3
  2.8 1.6 copy-start.4
  4.3 1.4 copy-start.1
  4.3 2.1 %copy-start.5 = (f32[128,32]{0,1:T(8,128)S(1)}, f32[128,32]{0,1:T(8,128)}, u32[]{:S(2)}) copy-start(f32[128,32]{0,1:T(8,128)} %param.11) | copy-start | bytes 49156
  181.8 2.9 %copy-start.2 = (bf16[8,2,4,64,128]{4,3,2,1,0:T(8,128)(2,1)S(1)}, bf16[8,2,4,64,128]{4,3,2,1,0:T(8,128)(2,1)}, u32[]{:S(2)}) copy-start(bf16[8,2,4,64,128]{4,3,2,1,0:T(8,128)(2,1)} %get-tuple-element.5) | copy-start | bytes 3145732

commit v2 on v0

v2 whole, which is shorter than its diff:
```python
import math
import jax
import jax.numpy as jnp
from jax import lax
from jax.experimental import pallas as pl
from jax.experimental.pallas import tpu as pltpu
from jax.sharding import PartitionSpec as P

f32, bf16 = jnp.float32, jnp.bfloat16
LOG2E = 1.4426950408889634
SCALE = 1.0 / math.sqrt(128.0)
NT = (((1,), (1,)), ((), ()))
TN = (((0,), (0,)), ((), ()))
MESH = pl.DeviceIdType.MESH
BOTH, NEAR, AROUND = (0, 1), (1, 3), (1, 3, 2)
STEPS = (("c1", "s3", "s1", "c3", "c2", "c0", "s2"), ("c1", "c3", "s1", "c2", "s3", "c0", "s2"))
PASS = ("00s3E9", "00s3L3+", "00s1E4", "00s1L5+", "00s2E12", "00s2L13",
        "12s1E4", "33s1E5", "11s1L5+", "22s1L6", "13s3E9", "11s2E12", "11s2L13", "23s2E13")

def _pick(k, values):
    r = values[0]
    for n in range(1, len(values)):
        r = jnp.where(k == n, values[n], r)
    return r


def _kernel(q_in, do_in, l_in, d_in, k_in, v_in, out_dq, out_dk, out_dv,
            qd, stb, st2, kv, dq, acc, rxy, rxz, rzf, dqx, dqs, dks,
            in_s, ql_r, fl_s, fl_r, kvg_s, kvg_r, ry_s, ry_r, rz_s, rz_r, odk_s, odk_r, dqx_s, dqx_r,
            kvo_r, st_r, qe_r, fe_s, fe_r, zf_s, zf_r, odq_s, odq_r):
    cy, cx = lax.axis_index("cy"), lax.axis_index("cx")
    rem, div = lax.rem, lax.div
    x, c = div(cx, 2), rem(cx, 2)
    yl, s = rem(cy, 2), div(cy, 2)
    z, bs = div(s, 2), rem(s, 2)
    a = rem(yl + bs, 2)
    i = yl * 4 + x
    h = a * 4 + x
    pair = 2 * z + 1 - bs

    def member(i2):
        yl2, x2 = div(i2, 4), rem(i2, 4)
        return {"cy": 2 * s + yl2, "cx": 2 * x2 + c}, rem(yl2 + bs, 2) * 4 + x2

    def peer(s2):
        return {"cy": 2 * s2 + rem(a + rem(s2, 2), 2), "cx": cx}

    across = peer(pair)
    partner = {"cy": cy, "cx": cx + 1 - 2 * c}
    others = [member(rem(i + t, 8)) for t in range(1, 8)]

    def block(el, i2):
        return pl.ds(pl.multiple_of((i2 + el * (7 - 2 * i2)) * 64, 64), 64)

    def half(cp, el):
        return pl.ds(pl.multiple_of(cp * 1024 + el * 512, 512), 512)

    def rows(cp, el, i2):
        return pl.ds(pl.multiple_of(cp * 1024 + el * 512 + (i2 + el * (7 - 2 * i2)) * 64, 64), 64)

    def remote(src, dst, ssem, rsem, dev):
        return pltpu.make_async_remote_copy(src, dst, ssem, rsem, device_id=dev, device_id_type=MESH)

    def arrived(ref, rsem):
        remote(ref, ref, in_s.at[0], rsem, partner).wait_recv()

    def sent(ref, ssem):
        remote(ref, ref, ssem, st_r.at[0], partner).wait_send()

    for el in BOTH:
        for n, src in enumerate((k_in, v_in)):
            pltpu.make_async_copy(src.at[h, el], kv.at[s, el, n, block(el, i), :], kvo_r.at[el]).start()
    for n, src in enumerate((l_in, d_in)):
        pltpu.make_async_copy(src.at[h], stb.at[c, i, n], st_r.at[0]).start()
    for n, src in enumerate((q_in, do_in)):
        for hh in range(4):
            pltpu.make_async_copy(src.at[h, 1, hh], qd.at[n, hh, rows(c, 1, i), :], ql_r.at[hh]).start()
        pltpu.make_async_copy(src.at[h, 0], qd.at[n, :, rows(c, 0, i), :], qe_r.at[0]).start()

    bar = pltpu.get_barrier_semaphore()
    pl.semaphore_signal(bar, inc=1, device_id=partner, device_id_type=MESH)
    pl.semaphore_signal(bar, inc=1, device_id=across, device_id_type=MESH)
    for dev, _ in others:
        pl.semaphore_signal(bar, inc=1, device_id=dev, device_id_type=MESH)
    for d in range(1, 4):
        pl.semaphore_signal(bar, inc=1, device_id=peer(2 * rem(z + d, 4) + bs), device_id_type=MESH)
    pl.semaphore_wait(bar, 12)

    for el in BOTH:
        for dev, h2 in others:
            for n, src in enumerate((k_in, v_in)):
                remote(src.at[h2, el], kv.at[s, el, n, block(el, i), :], in_s.at[n], kvo_r.at[el], dev).start()
    for dev, h2 in others:
        for n, src in enumerate((l_in, d_in)):
            remote(src.at[h2], stb.at[c, i, n], in_s.at[4 + n], st_r.at[0], dev).start()
    for hh in range(4):
        for dev, h2 in others:
            for n, src in enumerate((q_in, do_in)):
                remote(src.at[h2, 1, hh], qd.at[n, hh, rows(c, 1, i), :], in_s.at[2 + n], ql_r.at[hh], dev).start()
    for dev, h2 in others:
        for n, src in enumerate((q_in, do_in)):
            remote(src.at[h2, 0], qd.at[n, :, rows(c, 0, i), :], in_s.at[2 + n], qe_r.at[0], dev).start()

    def zero_acc(n, carry):
        acc[n] = jnp.zeros(acc.shape[1:], f32)
        return carry

    lax.fori_loop(0, 8, zero_acc, 0)
    for hh in range(4):
        dq[hh] = jnp.zeros(dq.shape[1:], f32)

    def spread(g, el, d, n):
        return remote(kv.at[g, el], kv.at[g, el], kvg_s.at[el, n], kvg_r.at[el, g], peer(2 * rem(z + 4 - d, 4) + bs))

    def spread_all(g, el, n0, ds, act):
        for d in ds:
            if el == 0:
                act(spread(g, el, d, n0 + d))
            else:
                pl.when(z > rem(z + 4 - d, 4))(lambda: act(spread(g, el, d, n0 + d)))

    def to_across(el):
        return remote(kv.at[s, el], kv.at[s, el], kvg_s.at[el, 0], kvg_r.at[el, s], across)

    def start(cp):
        cp.start()

    for el in BOTH:
        arrived(kv.at[s, el], kvo_r.at[el])
        to_across(el).start()
        spread_all(s, el, 0, NEAR, start)

    def build_stats(cp):
        for i2 in range(8):
            for n, factor in enumerate((LOG2E, 1.0)):
                tile = jnp.transpose(stb[cp, i2, n] * factor)
                for el in BOTH:
                    st2[rows(cp, el, i2), 4 * n:4 * n + 4] = tile[64 * el:64 * el + 64]

    st_fw = remote(stb.at[c], stb.at[c], fe_s.at[1], fe_r.at[1], partner)
    arrived(stb.at[c], st_r.at[0])
    st_fw.start()
    build_stats(c)

    def fw_late(hh):
        return remote(qd.at[:, hh, half(c, 1), :], qd.at[:, hh, half(c, 1), :], fl_s.at[hh], fl_r.at[hh], partner)

    def fw_early():
        return remote(qd.at[:, :, half(c, 0), :], qd.at[:, :, half(c, 0), :], fe_s.at[0], fe_r.at[0], partner)

    def scores(hh, r, kref, vref, nk, l2, d, mask=None):
        sc = lax.dot_general(qd[0, hh, r, :], kref[0:nk, :], NT, preferred_element_type=f32)
        dp = lax.dot_general(qd[1, hh, r, :], vref[0:nk, :], NT, preferred_element_type=f32)
        p = jnp.exp2(sc * (SCALE * LOG2E) - l2)
        if mask is not None:
            u, pq, pk = mask
            rr = lax.broadcasted_iota(jnp.int32, (256, nk), 0) + 256 * u
            kk = lax.broadcasted_iota(jnp.int32, (256, nk), 1)
            qpos = (rr >> 6) * 128 + (rr & 63) + pq * 64
            kpos = (kk >> 6) * 128 + (kk & 63) + pk * 64
            p = jnp.where(qpos >= kpos, p, 0.0)
        return p.astype(bf16), (p * (dp - d)).astype(bf16)

    def terms(hh, r, kref, dkref, dvref, nk, pb, ds):
        dkref[:, 0:nk] += lax.dot_general(qd[0, hh, r, :], ds, TN, preferred_element_type=f32)
        dvref[:, 0:nk] += lax.dot_general(qd[1, hh, r, :], pb, TN, preferred_element_type=f32)
        dq[hh, r, :] += jnp.dot(ds, kref[0:nk, :], preferred_element_type=f32)

    def pipelined(todo):
        now = todo[0][0]()
        for n in range(len(todo)):
            nxt = todo[n + 1][0]() if n + 1 < len(todo) else None
            todo[n][1](*now)
            now = nxt

    def tiles(bases, kref, vref, dkref, dvref, masks=None):
        def pair_of(n, hh, u):
            nk = 512 if masks is None or u == 1 else 256
            r = pl.ds(bases[n] + 256 * u, 256)
            mask = None if masks is None else (u, *masks[n])
            return (lambda: scores(hh, r, kref, vref, nk, st2[r, hh:hh + 1], st2[r, 4 + hh:5 + hh], mask),
                    lambda pb, ds: terms(hh, r, kref, dkref, dvref, nk, pb, ds))
        pipelined([pair_of(n, hh, u) for n in range(len(bases)) for u in range(2) for hh in range(4)])

    def heads_in(hh):
        arrived(qd.at[:, hh, half(c, 1), :], ql_r.at[hh])
        fw_late(hh).start()

    def partner_heads_in(hh):
        arrived(qd.at[:, hh, half(1 - c, 1), :], fl_r.at[hh])

    def own_tiles(hh, cp):
        r0 = pl.multiple_of(cp * 1024 + 512, 512)

        def pair_of(el, u):
            nk = 256 if el > u else 512
            r = pl.ds(r0 + 256 * u, 256)
            mask = None if el == 0 else (u, rem(cp + 1, 2), rem(c + 1, 2))
            kref, vref = kv.at[s, el, 0], kv.at[s, el, 1]

            def first():
                st = pltpu.roll(st2[r, :], rem(128 - hh, 128), 1)
                return scores(hh, r, kref, vref, nk, st[:, 0:1], st[:, 4:5], mask)

            return first, lambda pb, ds: terms(hh, r, kref, acc.at[0, el, 0], acc.at[0, el, 1], nk, pb, ds)

        pipelined([pair_of(el, u) for el in range(2) for u in range(2)])

    def own_unit(m, carry):
        hh, other = div(m, 2), rem(m, 2)

        @pl.when(other == 0)
        def _():
            heads_in(hh)

        @pl.when(m == 1)
        def _():
            arrived(stb.at[1 - c], fe_r.at[1])
            build_stats(1 - c)
            arrived(kv.at[pair, 0], kvg_r.at[0, pair])
            spread_all(pair, 0, 3, NEAR, start)

        @pl.when(m == 3)
        def _():
            arrived(kv.at[pair, 1], kvg_r.at[1, pair])
            spread_all(pair, 1, 3, NEAR, start)
            for el in BOTH:
                spread_all(s, el, 0, (2,), start)
                spread_all(pair, el, 3, (2,), start)

        @pl.when(other == 1)
        def _():
            partner_heads_in(hh)

        own_tiles(hh, rem(c + m, 2))
        return carry

    def late_heads(cp):
        lax.fori_loop(2, 4, lambda hh, carry: own_tiles(hh, cp), None)

    lax.fori_loop(0, 4, own_unit, 0)
    for hh in (2, 3):
        heads_in(hh)
    late_heads(c)
    for hh in (2, 3):
        partner_heads_in(hh)

    def acc_y(k, d, kel):
        return remote(acc.at[k + 1, kel], rxy.at[d, kel], ry_s.at[kel, d], ry_r.at[kel, d], across)

    def acc_z(k, d, kel):
        return remote(acc.at[k + 1, kel], rxz.at[z, kel], rz_s.at[kel, d], rz_r.at[kel, z], peer(2 * rem(z + d, 4) + bs))

    def acc_f(k, d):
        return remote(acc.at[k + 1, 1], rzf, zf_s.at[rem(d, 2) * div(d, 2)], zf_r.at[0], peer(2 * rem(z + d, 4) + bs))

    def by_z_first(d):
        return ((z == 0) & (rem(d, 2) == 1)) | ((z == 1) & (d == 1))

    def step_of(k):
        d, cross = (jnp.where(z == 0, *(_pick(k, [of(name) for name in order]) for order in STEPS))
                    for of in (lambda name: int(name[1]), lambda name: int(name[0] == "c")))
        g = 2 * rem(z + d, 4) + rem(bs + cross, 2)
        return d, cross, g, div(g - s + 7, 8)

    def pass_at(n):
        for entry in PASS:
            z_lo, z_hi, d, kel = int(entry[0]), int(entry[1]), int(entry[3]), "EL".index(entry[4])
            k = STEPS[min(z_lo, 1)].index(entry[2:4])

            def go_on():
                if not entry.endswith("+"):
                    arrived(rxy.at[d, kel], ry_r.at[kel, d])
                    acc[k + 1, kel] += rxy[d, kel]
                acc_z(k, d, kel).start()

            pl.when((n == int(entry[5:].rstrip("+"))) & (z >= z_lo) & (z <= z_hi))(go_on)

    def late_across(k, d):
        zfirst = by_z_first(d)

        @pl.when(zfirst)
        def _():
            acc_f(k, d).start()

        @pl.when((d == 0) & (z > 0))
        def _():
            arrived(rzf, zf_r.at[0])
            acc[k + 1, 1] += rzf[...]

        @pl.when(jnp.logical_not(zfirst))
        def _():
            acc_y(k, d, 1).start()

    def full_unit(n, carry):
        k, sub = div(n, 2), rem(n, 2)
        d, cross, g, gt = step_of(k)
        el = 1 - sub + sub * gt
        kel = sub * gt

        last = div(z, 3)

        @pl.when(n == 2 - last)
        def _():
            pl.when(z == 3)(lambda: late_heads(1 - c))
            arrived(qd.at[:, :, half(c, 0), :], qe_r.at[0])
            fw_early().start()

        @pl.when(n == 3 - 2 * last)
        def _():
            arrived(qd.at[:, :, half(1 - c, 0), :], fe_r.at[0])

        @pl.when((sub == 0) & (d > 0))
        def _():
            arrived(kv.at[g, 0], kvg_r.at[0, g])

        @pl.when((sub == 1) & (d > 0) & (gt == 1))
        def _():
            arrived(kv.at[g, 1], kvg_r.at[1, g])

        bases = [pl.multiple_of(cp * 1024 + el * 512, 512) for cp in (c, 1 - c)]
        tiles(bases, kv.at[g, kel, 0], kv.at[g, kel, 1], acc.at[k + 1, kel, 0], acc.at[k + 1, kel, 1])

        @pl.when((cross == 1) & (sub == gt) & ((gt == 1) | ((d == 0) & (z > 0))))
        def _():
            late_across(k, d)

        @pl.when((cross == 1) & (sub == 1 - gt))
        def _():
            acc_y(k, d, 0).start()

        pass_at(n)
        return carry

    lax.fori_loop(0, 14, full_unit, 0)

    def heads(p):
        return pl.ds(2 * p, 2)

    def dqx_copy(el, p):
        return remote(dq.at[heads(p), half(1 - c, el), :], dqx.at[el, heads(p)], dqx_s.at[el, p], dqx_r.at[el, p], partner)

    def finish_dq(el, p):
        arrived(dqx.at[el, heads(p)], dqx_r.at[el, p])
        for hh in (2 * p, 2 * p + 1):
            dqs[el, hh] = ((dq[hh, half(c, el), :] + dqx[el, hh]) * SCALE).astype(bf16)
        out = out_dq.at[h, heads(p), el]
        for t, (dev, _) in enumerate(others):
            remote(dqs.at[el, heads(p), block(el, rem(i + t + 1, 8)), :], out, odq_s.at[el], odq_r.at[el], dev).start()
        pltpu.make_async_copy(dqs.at[el, heads(p), block(el, i), :], out, odq_r.at[el]).start()

    dqx_copy(1, 0).start()

    def diag_unit(m, carry):
        cp = rem(c + 1 + m, 2)
        kd, vd = kv.at[s, 0, 0], kv.at[s, 0, 1]
        tiles([pl.multiple_of(cp * 1024, 512)], kd, vd, acc.at[0, 0, 0], acc.at[0, 0, 1], [(cp, c)])

        @pl.when(m == 0)
        def _():
            for p in BOTH:
                dqx_copy(0, p).start()
            finish_dq(1, 0)

        return carry

    lax.fori_loop(0, 2, diag_unit, 0)
    for p in BOTH:
        finish_dq(0, p)
    pl.when(z < 3)(lambda: late_heads(1 - c))
    dqx_copy(1, 1).start()
    finish_dq(1, 1)

    def take(ref, rsem, el):
        arrived(ref, rsem)
        acc[0, el] += ref[...]

    for el in BOTH:
        for d in AROUND:
            zs = rem(z + d, 4)

            def take_z():
                take(rxz.at[zs, el], rz_r.at[el, zs], el)

            take_z() if el == 0 else pl.when(z > zs)(take_z)

        def take_y():
            take(rxy.at[0, el], ry_r.at[el, 0], el)

        take_y() if el == 0 else pl.when((bs == 1) | (z > 0))(take_y)
        dks[el, 0] = (jnp.transpose(acc[0, el, 0]) * SCALE).astype(bf16)
        dks[el, 1] = jnp.transpose(acc[0, el, 1]).astype(bf16)
        for n, out in enumerate((out_dk, out_dv)):
            for t, (dev, _) in enumerate(others):
                remote(dks.at[el, n, block(el, rem(i + t + 1, 8)), :], out.at[h, el], odk_s.at[el, n], odk_r.at[el, n], dev).start()
            pltpu.make_async_copy(dks.at[el, n, block(el, i), :], out.at[h, el], odk_r.at[el, n]).start()

    for n, src in enumerate((k_in, v_in, q_in, do_in, l_in, d_in)):
        sent(src.at[pl.ds(0, 7)], in_s.at[n])
    for el in BOTH:
        to_across(el).wait_send()
        spread_all(s, el, 0, AROUND, lambda cp: cp.wait_send())
        spread_all(pair, el, 3, AROUND, lambda cp: cp.wait_send())
    st_fw.wait_send()
    fw_early().wait_send()
    for hh in range(4):
        fw_late(hh).wait_send()
    for k, name in enumerate(STEPS[0]):
        d, cross = int(name[1]), int(name[0] == "c")
        made = acc_y if cross else acc_z
        made(k, d, 0).wait_send()
        later = 2 * rem(z + d, 4) + rem(bs + cross, 2) > s
        if not cross:
            pl.when(later)(lambda: made(k, d, 1).wait_send())
        elif d == 0:
            pl.when(later | (z > 0))(lambda: made(k, d, 1).wait_send())
        else:
            zfirst = by_z_first(d)
            pl.when(zfirst)(lambda: acc_f(k, d).wait_send())
            pl.when(later & jnp.logical_not(zfirst))(lambda: made(k, d, 1).wait_send())
    for el in BOTH:
        for p in BOTH:
            dqx_copy(el, p).wait_send()
        sent(dqs.at[el, :, pl.ds(0, 448), :], odq_s.at[el])
        arrived(out_dq.at[:, :, el], odq_r.at[el])
        for n, out in enumerate((out_dk, out_dv)):
            sent(dks.at[el, n, pl.ds(0, 448), :], odk_s.at[el, n])
            arrived(out.at[:, el], odk_r.at[el, n])


def solution(mesh):
    row_spec = P(('dp', 'cy', 'cx'), None, None)
    stat_spec = P(('dp', 'cy', 'cx'), None)

    def local(q, k, v, o, do, lse):
        T, H, D = q.shape
        G = k.shape[1]
        R = H // G
        half = T // 2
        delta = jnp.sum(do.astype(f32) * o.astype(f32), axis=-1)
        l_in, d_in = (t.T.reshape(G, R, T) for t in (lse, delta))
        q_in, do_in = (t.reshape(2, half, G, R, D).transpose(2, 0, 3, 1, 4) for t in (q, do))
        k_in, v_in = (t.reshape(2, half, G, D).transpose(2, 0, 1, 3) for t in (k, v))
        hbm = pl.BlockSpec(memory_space=pl.ANY)
        V, S = pltpu.VMEM, pltpu.SemaphoreType.DMA
        S2, W = 2 * G * T, G * half
        dq_o, dk_o, dv_o = pl.pallas_call(
            _kernel,
            in_specs=[hbm] * 6,
            out_specs=[hbm] * 3,
            out_shape=[jax.ShapeDtypeStruct((G, R, 2, half, D), bf16)] + [jax.ShapeDtypeStruct((G, 2, half, D), bf16)] * 2,
            scratch_shapes=[
                V((2, R, S2, D), bf16), V((2, G, 2, R, T), f32), V((S2, T), f32), V((G, 2, 2, W, D), bf16), V((R, S2, D), f32),
                V((G, 2, 2, D, W), f32), V((4, 2, 2, D, W), f32), V((4, 2, 2, D, W), f32), V((2, D, W), f32), V((2, R, W, D), f32),
                V((2, R, W, D), bf16), V((2, 2, W, D), bf16),
                *[S((G,))] * 4, *[S((2, G))] * 10, *[S((2,))] * 9,
            ],
            compiler_params=pltpu.CompilerParams(collective_id=0, has_side_effects=True, vmem_limit_bytes=60 << 20),
            cost_estimate=pl.CostEstimate(flops=46 << 30, bytes_accessed=8 << 20, transcendentals=36 << 20),
            name="attn_bwd",
        )(q_in, do_in, l_in, d_in, k_in, v_in)
        grad_q = dq_o.reshape(H, T, D).transpose(1, 0, 2)
        grad_k, grad_v = (t.reshape(G, T, D).transpose(1, 0, 2) for t in (dk_o, dv_o))
        return grad_q, grad_k, grad_v

    return jax.shard_map(local, mesh=mesh, in_specs=(row_spec,) * 5 + (stat_spec,), out_specs=(row_spec,) * 3, check_vma=False)
```

time: 5130 us -> 143 us (0.03)
  waiting for transfers between devices: 3180 us -> 0 us
  other arithmetic: 984 us -> 2.27 us
  local copies, waits for them, and re-layouts: 525 us -> 9.01 us
  matrix products: 373 us -> 0 us
  Pallas kernels: 0 us -> 131 us
    ppermute x510 -> x0, waiting for transfers between devices: 3180 us -> none  [the longest x127 3110 us: step_body(): k_cur = lax.ppermute(k_cur, ctx_axes, shift_perm)]
    add x382 -> x0, other arithmetic: 981 us -> none  [the longest x381 981 us: step_body(): return (k_cur, v_cur, dk_cur + dk_part, dv_cur + dv_part, dq_cur + dq_part)]
    dot_general x640 -> x0, matrix products: 373 us -> none  [the longest x128 170 us: block_grads(): jnp.einsum('qkgd,skd->kqgs', do_blk, v_blk, preferred_element_type=jnp.fl...]
    while x258 -> x0, local copies, waits for them, and re-layouts: 305 us -> none
    concatenate x128 -> x0, local copies, waits for them, and re-layouts: 197 us -> none  [the longest x126 196 us: src_after(): return (jnp.concatenate([zero_pad, dq_part], axis=1), dk_part, dv_part)]
    pallas_call x0 -> x1, Pallas kernels: none -> 131 us  [local(): pl.pallas_call(_kernel, in_specs=[hbm] * 6, out_specs=[hbm] * 3, out_shap...]
  transfers between devices with their start and end apart: 510 -> 0, of which waited for: 255 -> 0; matrix products, arithmetic and copies ran while one was open for 32% -> 0% of each run, Pallas kernels for 0% -> 0%
where the time goes in v2:
time: 143 us
  Pallas kernels  131 us (92%)
  local copies, waits for them, and re-layouts  9.01 us (6%)
  other arithmetic  2.27 us (2%)
    pallas_call x1, Pallas kernels, local(): pl.pallas_call(_kernel, in_specs=[hbm] * 6, out_specs=[hbm] * 3, out_shap...  131 us
    reshape x1, local copies, waits for them, and re-layouts, local(): grad_q = dq_o.reshape(H, T, D).transpose(1, 0, 2)  2.93 us

profile of v2, /device:TPU:1, one launch (start us, length us, event | category | flops | bytes accessed | tf_op | source)
XLA Modules:
  0.0 142.6 jit_solution(4949031516812991104)
XLA Ops:
  0.6 0.0 copy-start.2
  0.6 0.0 copy-start.3
  0.7 0.0 copy-start.1
  0.7 2.3 %multiply_reduce_fusion = f32[128,32]{1,0:T(8,128)S(1)} fusion(bf16[128,32,128]{2,1,0:T(8,128)(2,1)} %param.9, bf16[128,32,128]{2,1,0:T(8,128)(2,1)} %param.10), kind=kLoop, calls=%fused_computation | loop fusion | flops 2093056 | bytes 2113536 | tf_op jit(solution)/shard_map/reduce_sum | solution.py:440
  2.9 0.0 copy-start
  2.9 0.7 copy.27
  3.6 0.0 copy-done.2
  3.6 0.7 copy.28
  4.4 0.0 copy-done.3
  4.4 0.7 copy.29
  5.1 0.0 copy-done.1
  5.1 0.0 copy-done
  5.1 2.1 %copy_bitcast_fusion = (bf16[8,2,4,64,128]{4,3,2,1,0:T(8,128)(2,1)}, bf16[8,2,4,64,128]{4,3,2,1,0:T(8,128)(2,1)}) fusion(bf16[2,64,8,4,128]{4,3,2,1,0:T(4,128)(2,1)S(1)} %bitcast.29, bf16[2,64,8,4,128]{4,3,2,1,0:T(4,128)(2,1)S(1)} %bitcast.32), kind=kLoop, calls=%fused_computation.1 | loop fusion | bytes 4194304 | tf_op jit(solution)/shard_map/transpose | solution.py:442
  7.3 130.6 %attn_bwd.1 = (bf16[8,4,2,64,128]{4,3,2,1,0:T(8,128)(2,1)}, bf16[8,2,64,128]{3,2,1,0:T(8,128)(2,1)}, bf16[8,2,64,128]{3,2,1,0:T(8,128)(2,1)}) custom-call(bf16[8,2,4,64,128]{4,3,2,1,0:T(8,128)(2,1)} %get-tuple-element.10.q_in, bf16[8,2,4,64,128]{4,3,2,1,0:T(8,128)(2,1)} %get-tuple-element.9.do_in, f32[8,4,128]{2,1,0:T(4,128)} %bitcast.41, ...), custom_call_target="tpu_custom_call" | custom-call | flops 49392123904 | bytes 8388608 | tf_op jit(solution)/shard_map/attn_bwd/pallas_call | solution.py:447
  137.8 0.0 copy-start.5
  137.9 0.0 copy-start.4
  137.9 2.9 %copy.42 = bf16[32,128,128]{2,0,1:T(8,128)(2,1)} copy(bf16[32,128,128]{2,1,0:T(8,128)(2,1)} %bitcast.31) | data formatting | bytes 2097152 | tf_op jit(solution)/shard_map/reshape | solution.py:462
  140.8 0.0 copy-done.5
  140.8 0.9 copy.44
  141.7 0.0 copy-done.4
  141.7 0.9 copy.43
Async XLA Ops:
  0.6 3.0 %copy-start.2 = (bf16[128,8,128]{2,1,0:T(8,128)(2,1)S(1)}, bf16[128,8,128]{2,1,0:T(8,128)(2,1)}, u32[]{:S(2)}) copy-start(bf16[128,8,128]{2,1,0:T(8,128)(2,1)} %param.7) | copy-start | bytes 786436
  0.6 3.7 %copy-start.3 = (bf16[128,8,128]{2,1,0:T(8,128)(2,1)S(1)}, bf16[128,8,128]{2,1,0:T(8,128)(2,1)}, u32[]{:S(2)}) copy-start(bf16[128,8,128]{2,1,0:T(8,128)(2,1)} %param.8) | copy-start | bytes 786436
  0.7 4.5 %copy-start.1 = (bf16[128,32,128]{2,1,0:T(8,128)(2,1)S(1)}, bf16[128,32,128]{2,1,0:T(8,128)(2,1)}, u32[]{:S(2)}) copy-start(bf16[128,32,128]{2,1,0:T(8,128)(2,1)} %param.6) | copy-start | bytes 3145732
  2.9 2.2 %copy-start = (bf16[128,32,128]{2,1,0:T(8,128)(2,1)S(1)}, bf16[128,32,128]{2,1,0:T(8,128)(2,1)}, u32[]{:S(2)}) copy-start(bf16[128,32,128]{2,1,0:T(8,128)(2,1)} %param.10) | copy-start | bytes 3145732
  137.8 3.0 %copy-start.5 = (bf16[8,2,64,128]{3,2,1,0:T(8,128)(2,1)S(1)}, bf16[8,2,64,128]{3,2,1,0:T(8,128)(2,1)}, u32[]{:S(2)}) copy-start(bf16[8,2,64,128]{3,2,1,0:T(8,128)(2,1)} %get-tuple-element.7) | copy-start | bytes 786436
  137.9 3.8 %copy-start.4 = (bf16[8,2,64,128]{3,2,1,0:T(8,128)(2,1)S(1)}, bf16[8,2,64,128]{3,2,1,0:T(8,128)(2,1)}, u32[]{:S(2)}) copy-start(bf16[8,2,64,128]{3,2,1,0:T(8,128)(2,1)} %get-tuple-element.8) | copy-start | bytes 786436

commit v3 on v2

--- a/solution.py
+++ b/solution.py
@@ -13,9 +13,9 @@
 TN = (((0,), (0,)), ((), ()))
 MESH = pl.DeviceIdType.MESH
 BOTH, NEAR, AROUND = (0, 1), (1, 3), (1, 3, 2)
-STEPS = (("c1", "s3", "s1", "c3", "c2", "c0", "s2"), ("c1", "c3", "s1", "c2", "s3", "c0", "s2"))
-PASS = ("00s3E9", "00s3L3+", "00s1E4", "00s1L5+", "00s2E12", "00s2L13",
-        "12s1E4", "33s1E5", "11s1L5+", "22s1L6", "13s3E9", "11s2E12", "11s2L13", "23s2E13")
+STEPS = (("c1", "s1", "s3", "c3", "c2", "c0", "s2"), ("c1", "c3", "s1", "c2", "s3", "c0", "s2"), ("c1", "c3", "s1", "c2", "s2", "c0", "s3"))
+PASS = ("00s3E9", "00s3L5+", "00s1E4", "00s1L3+", "00s2E12", "00s2L14",
+        "12s1E4", "33s1E5", "11s1L5+", "22s1L6", "11s3E9", "11s2E12", "11s2L13", "23s2E10", "23s3E13")
 
 def _pick(k, values):
     r = values[0]
@@ -24,11 +24,13 @@
     return r
 
 
-def _kernel(q_in, do_in, l_in, d_in, k_in, v_in, out_dq, out_dk, out_dv,
-            qd, stb, st2, kv, dq, acc, rxy, rxz, rzf, dqx, dqs, dks,
+def _kernel(q, do, o, k, v, l_in, out_dq, out_dk, out_dv,
+            qn, don, on, kn, vn, wide_q, wide_o, q_in, do_in, k_in, v_in, d_in, dqr, dkr, dvr,
+            qd, stb, st2, kv, dq, acc, rxy, rxz, rzf, dqx, dqs, dks, nat_s,
             in_s, ql_r, fl_s, fl_r, kvg_s, kvg_r, ry_s, ry_r, rz_s, rz_r, odk_s, odk_r, dqx_s, dqx_r,
-            kvo_r, st_r, qe_r, fe_s, fe_r, zf_s, zf_r, odq_s, odq_r):
+            loc_s, kvo_r, st_r, qe_r, fe_s, fe_r, zf_s, zf_r, odq_s, odq_r):
     cy, cx = lax.axis_index("cy"), lax.axis_index("cx")
+    T = q.shape[0]
     rem, div = lax.rem, lax.div
     x, c = div(cx, 2), rem(cx, 2)
     yl, s = rem(cy, 2), div(cy, 2)
@@ -48,6 +50,7 @@
     across = peer(pair)
     partner = {"cy": cy, "cx": cx + 1 - 2 * c}
     others = [member(rem(i + t, 8)) for t in range(1, 8)]
+    seven = pl.ds(0, 7 * 64)
 
     def block(el, i2):
         return pl.ds(pl.multiple_of((i2 + el * (7 - 2 * i2)) * 64, 64), 64)
@@ -67,15 +70,10 @@
     def sent(ref, ssem):
         remote(ref, ref, ssem, st_r.at[0], partner).wait_send()
 
-    for el in BOTH:
-        for n, src in enumerate((k_in, v_in)):
-            pltpu.make_async_copy(src.at[h, el], kv.at[s, el, n, block(el, i), :], kvo_r.at[el]).start()
-    for n, src in enumerate((l_in, d_in)):
-        pltpu.make_async_copy(src.at[h], stb.at[c, i, n], st_r.at[0]).start()
-    for n, src in enumerate((q_in, do_in)):
-        for hh in range(4):
-            pltpu.make_async_copy(src.at[h, 1, hh], qd.at[n, hh, rows(c, 1, i), :], ql_r.at[hh]).start()
-        pltpu.make_async_copy(src.at[h, 0], qd.at[n, :, rows(c, 0, i), :], qe_r.at[0]).start()
+    natives = [pltpu.make_async_copy(src, dst, nat_s.at[n]) for n, (src, dst) in enumerate(((k, kn), (v, vn), (q, qn), (do, don), (o, on)))]
+    for cp_ in natives:
+        cp_.start()
+    pltpu.make_async_copy(l_in.at[h], stb.at[c, i, 0], loc_s.at[0]).start()
 
     bar = pltpu.get_barrier_semaphore()
     pl.semaphore_signal(bar, inc=1, device_id=partner, device_id_type=MESH)
@@ -84,30 +82,56 @@
         pl.semaphore_signal(bar, inc=1, device_id=dev, device_id_type=MESH)
     for d in range(1, 4):
         pl.semaphore_signal(bar, inc=1, device_id=peer(2 * rem(z + d, 4) + bs), device_id_type=MESH)
+
+    def widen(ref, wide):
+        heads_ = ref.shape[1]
+        for t in range(0, ref.shape[0], 16):
+            wide[pl.ds(t * heads_, 16 * heads_), :] = ref[pl.ds(t, 16)].astype(f32).reshape(16 * heads_, ref.shape[2])
+
+    def of_head(wide, j, heads_):
+        return wide[pl.ds(j, T, stride=heads_), :]
+
+    for n, (ref, dst) in enumerate(((kn, k_in), (vn, v_in))):
+        natives[n].wait()
+        widen(ref, wide_o)
+        for j in range(8):
+            rows_ = of_head(wide_o, j, 8).astype(bf16)
+            for el in BOTH:
+                dst[j, el] = rows_[64 * el:64 * el + 64]
+        for el in BOTH:
+            kv[s, el, n, block(el, i), :] = dst[h, el]
+    def by_head(n, ref, dst, stats):
+        natives[2 + n].wait()
+        widen(ref, wide_q)
+        if stats:
+            natives[4].wait()
+            widen(on, wide_o)
+        for j in range(32):
+            rows_ = of_head(wide_q, j, 32)
+            for el in BOTH:
+                dst[j // 4, el, j % 4] = rows_[64 * el:64 * el + 64].astype(bf16)
+            if stats:
+                terms_ = rows_ * of_head(wide_o, j, 32)
+                d_in[j // 4, pl.ds(j % 4, 1), :] = jnp.sum(jnp.transpose(terms_), axis=0, keepdims=True)
+        for el in BOTH:
+            qd[n, :, rows(c, el, i), :] = dst[h, el]
+
+    by_head(0, qn, q_in, False)
+    def zero_acc(n, carry):
+        acc[n] = jnp.zeros(acc.shape[1:], f32)
+        return carry
+
+    lax.fori_loop(0, 8, zero_acc, 0)
+    for hh in range(4):
+        dq[hh] = jnp.zeros(dq.shape[1:], f32)
+
     pl.semaphore_wait(bar, 12)
-
     for el in BOTH:
         for dev, h2 in others:
             for n, src in enumerate((k_in, v_in)):
                 remote(src.at[h2, el], kv.at[s, el, n, block(el, i), :], in_s.at[n], kvo_r.at[el], dev).start()
-    for dev, h2 in others:
-        for n, src in enumerate((l_in, d_in)):
-            remote(src.at[h2], stb.at[c, i, n], in_s.at[4 + n], st_r.at[0], dev).start()
-    for hh in range(4):
-        for dev, h2 in others:
-            for n, src in enumerate((q_in, do_in)):
-                remote(src.at[h2, 1, hh], qd.at[n, hh, rows(c, 1, i), :], in_s.at[2 + n], ql_r.at[hh], dev).start()
-    for dev, h2 in others:
-        for n, src in enumerate((q_in, do_in)):
-            remote(src.at[h2, 0], qd.at[n, :, rows(c, 0, i), :], in_s.at[2 + n], qe_r.at[0], dev).start()
-
-    def zero_acc(n, carry):
-        acc[n] = jnp.zeros(acc.shape[1:], f32)
-        return carry
-
-    lax.fori_loop(0, 8, zero_acc, 0)
-    for hh in range(4):
-        dq[hh] = jnp.zeros(dq.shape[1:], f32)
+    by_head(1, don, do_in, True)
+    stb[c, i, 1] = d_in[h]
 
     def spread(g, el, d, n):
         return remote(kv.at[g, el], kv.at[g, el], kvg_s.at[el, n], kvg_r.at[el, g], peer(2 * rem(z + 4 - d, 4) + bs))
@@ -125,10 +149,29 @@
     def start(cp):
         cp.start()
 
-    for el in BOTH:
-        arrived(kv.at[s, el], kvo_r.at[el])
+    def send_stats():
+        for dev, h2 in others:
+            for n, src in enumerate((l_in, d_in)):
+                remote(src.at[h2], stb.at[c, i, n], in_s.at[4 + n], st_r.at[0], dev).start()
+
+    def send_late():
+        for hh in range(4):
+            for dev, h2 in others:
+                for n, src in enumerate((q_in, do_in)):
+                    remote(src.at[h2, 1, hh], qd.at[n, hh, rows(c, 1, i), :], in_s.at[2 + n], ql_r.at[hh], dev).start()
+
+    def send_early():
+        for dev, h2 in others:
+            for n, src in enumerate((q_in, do_in)):
+                remote(src.at[h2, 0], qd.at[n, :, rows(c, 0, i), :], in_s.at[2 + n], qe_r.at[0], dev).start()
+
+    for el in BOTH:
+        arrived(kv.at[s, el, :, seven], kvo_r.at[el])
         to_across(el).start()
-        spread_all(s, el, 0, NEAR, start)
+        spread_all(s, el, 0, NEAR if el == 0 else (3,), start)
+        if el == 0:
+            send_stats()
+            send_late()
 
     def build_stats(cp):
         for i2 in range(8):
@@ -138,7 +181,8 @@
                     st2[rows(cp, el, i2), 4 * n:4 * n + 4] = tile[64 * el:64 * el + 64]
 
     st_fw = remote(stb.at[c], stb.at[c], fe_s.at[1], fe_r.at[1], partner)
-    arrived(stb.at[c], st_r.at[0])
+    arrived(stb.at[c, pl.ds(0, 7)], st_r.at[0])
+    pltpu.make_async_copy(l_in.at[h], stb.at[c, i, 0], loc_s.at[0]).wait()
     st_fw.start()
     build_stats(c)
 
@@ -183,7 +227,7 @@
         pipelined([pair_of(n, hh, u) for n in range(len(bases)) for u in range(2) for hh in range(4)])
 
     def heads_in(hh):
-        arrived(qd.at[:, hh, half(c, 1), :], ql_r.at[hh])
+        arrived(qd.at[:, hh, seven], ql_r.at[hh])
         fw_late(hh).start()
 
     def partner_heads_in(hh):
@@ -224,6 +268,7 @@
         def _():
             arrived(kv.at[pair, 1], kvg_r.at[1, pair])
             spread_all(pair, 1, 3, NEAR, start)
+            spread_all(s, 1, 0, (1,), start)
             for el in BOTH:
                 spread_all(s, el, 0, (2,), start)
                 spread_all(pair, el, 3, (2,), start)
@@ -238,6 +283,7 @@
     def late_heads(cp):
         lax.fori_loop(2, 4, lambda hh, carry: own_tiles(hh, cp), None)
 
+    send_early()
     lax.fori_loop(0, 4, own_unit, 0)
     for hh in (2, 3):
         heads_in(hh)
@@ -258,7 +304,7 @@
         return ((z == 0) & (rem(d, 2) == 1)) | ((z == 1) & (d == 1))
 
     def step_of(k):
-        d, cross = (jnp.where(z == 0, *(_pick(k, [of(name) for name in order]) for order in STEPS))
+        d, cross = (_pick(z, [_pick(k, [of(name) for name in order]) for order in (*STEPS, STEPS[2])])
                     for of in (lambda name: int(name[1]), lambda name: int(name[0] == "c")))
         g = 2 * rem(z + d, 4) + rem(bs + cross, 2)
         return d, cross, g, div(g - s + 7, 8)
@@ -266,7 +312,7 @@
     def pass_at(n):
         for entry in PASS:
             z_lo, z_hi, d, kel = int(entry[0]), int(entry[1]), int(entry[3]), "EL".index(entry[4])
-            k = STEPS[min(z_lo, 1)].index(entry[2:4])
+            k = STEPS[min(z_lo, 2)].index(entry[2:4])
 
             def go_on():
                 if not entry.endswith("+"):
@@ -292,6 +338,20 @@
         def _():
             acc_y(k, d, 1).start()
 
+    def heads(p):
+        return pl.ds(2 * p, 2)
+
+    def dqx_copy(el, p):
+        return remote(dq.at[heads(p), half(1 - c, el), :], dqx.at[el, heads(p)], dqx_s.at[el, p], dqx_r.at[el, p], partner)
+
+    def finish_dq(el, p):
+        arrived(dqx.at[el, heads(p)], dqx_r.at[el, p])
+        for hh in (2 * p, 2 * p + 1):
+            dqs[el, hh] = ((dq[hh, half(c, el), :] + dqx[el, hh]) * SCALE).astype(bf16)
+        for t, (dev, _) in enumerate(others):
+            remote(dqs.at[el, heads(p), block(el, rem(i + t + 1, 8)), :], dqr.at[h, heads(p), el], odq_s.at[el], odq_r.at[el], dev).start()
+        dqr[h, heads(p), el] = dqs[el, heads(p), block(el, i), :]
+
     def full_unit(n, carry):
         k, sub = div(n, 2), rem(n, 2)
         d, cross, g, gt = step_of(k)
@@ -303,7 +363,7 @@
         @pl.when(n == 2 - last)
         def _():
             pl.when(z == 3)(lambda: late_heads(1 - c))
-            arrived(qd.at[:, :, half(c, 0), :], qe_r.at[0])
+            arrived(qd.at[:, :, seven], qe_r.at[0])
             fw_early().start()
 
         @pl.when(n == 3 - 2 * last)
@@ -330,26 +390,20 @@
             acc_y(k, d, 0).start()
 
         pass_at(n)
+
+        @pl.when(n == 13 - div(z, 2))
+        def _():
+            dqx_copy(1, 0).start()
+            pl.when(z == 3)(lambda: dqx_copy(1, 1).start())
+
         return carry
 
     lax.fori_loop(0, 14, full_unit, 0)
 
-    def heads(p):
-        return pl.ds(2 * p, 2)
-
-    def dqx_copy(el, p):
-        return remote(dq.at[heads(p), half(1 - c, el), :], dqx.at[el, heads(p)], dqx_s.at[el, p], dqx_r.at[el, p], partner)
-
-    def finish_dq(el, p):
-        arrived(dqx.at[el, heads(p)], dqx_r.at[el, p])
-        for hh in (2 * p, 2 * p + 1):
-            dqs[el, hh] = ((dq[hh, half(c, el), :] + dqx[el, hh]) * SCALE).astype(bf16)
-        out = out_dq.at[h, heads(p), el]
-        for t, (dev, _) in enumerate(others):
-            remote(dqs.at[el, heads(p), block(el, rem(i + t + 1, 8)), :], out, odq_s.at[el], odq_r.at[el], dev).start()
-        pltpu.make_async_copy(dqs.at[el, heads(p), block(el, i), :], out, odq_r.at[el]).start()
-
-    dqx_copy(1, 0).start()
+    @pl.when(z >= 2)
+    def _():
+        finish_dq(1, 0)
+        pl.when(z == 3)(lambda: finish_dq(1, 1))
 
     def diag_unit(m, carry):
         cp = rem(c + 1 + m, 2)
@@ -360,16 +414,21 @@
         def _():
             for p in BOTH:
                 dqx_copy(0, p).start()
-            finish_dq(1, 0)
+            pass_at(14)
+            pl.when(z < 2)(lambda: finish_dq(1, 0))
 
         return carry
 
     lax.fori_loop(0, 2, diag_unit, 0)
     for p in BOTH:
         finish_dq(0, p)
-    pl.when(z < 3)(lambda: late_heads(1 - c))
-    dqx_copy(1, 1).start()
-    finish_dq(1, 1)
+
+    @pl.when(z < 3)
+    def _():
+        late_heads(1 - c)
+        dqx_copy(1, 1).start()
+        finish_dq(1, 1)
+
 
     def take(ref, rsem, el):
         arrived(ref, rsem)
@@ -390,10 +449,24 @@
         take_y() if el == 0 else pl.when((bs == 1) | (z > 0))(take_y)
         dks[el, 0] = (jnp.transpose(acc[0, el, 0]) * SCALE).astype(bf16)
         dks[el, 1] = jnp.transpose(acc[0, el, 1]).astype(bf16)
-        for n, out in enumerate((out_dk, out_dv)):
+        for n, got in enumerate((dkr, dvr)):
             for t, (dev, _) in enumerate(others):
-                remote(dks.at[el, n, block(el, rem(i + t + 1, 8)), :], out.at[h, el], odk_s.at[el, n], odk_r.at[el, n], dev).start()
-            pltpu.make_async_copy(dks.at[el, n, block(el, i), :], out.at[h, el], odk_r.at[el, n]).start()
+                remote(dks.at[el, n, block(el, rem(i + t + 1, 8)), :], got.at[h, el], odk_s.at[el, n], odk_r.at[el, n], dev).start()
+            got[h, el] = dks[el, n, block(el, i), :]
+
+    def by_token(got, el, heads_, wide, out):
+        for j in range(heads_):
+            wide[pl.ds(j + 64 * el * heads_, 64, stride=heads_), :] = got(j).astype(f32)
+        for t in range(64 * el, 64 * el + 64, 16):
+            out[pl.ds(t, 16)] = wide[pl.ds(t * heads_, 16 * heads_), :].reshape(16, heads_, out.shape[2]).astype(bf16)
+
+    for el in BOTH:
+        arrived(dqr.at[pl.ds(0, 7), :, el], odq_r.at[el])
+        by_token(lambda j: dqr[j // 4, j % 4, el], el, 32, wide_q, out_dq)
+    for el in BOTH:
+        for n, (got, out) in enumerate(((dkr, out_dk), (dvr, out_dv))):
+            arrived(got.at[pl.ds(0, 7), el], odk_r.at[el, n])
+            by_token(lambda j: got[j, el], el, 8, wide_o, out)
 
     for n, src in enumerate((k_in, v_in, q_in, do_in, l_in, d_in)):
         sent(src.at[pl.ds(0, 7)], in_s.at[n])
@@ -422,10 +495,8 @@
         for p in BOTH:
             dqx_copy(el, p).wait_send()
         sent(dqs.at[el, :, pl.ds(0, 448), :], odq_s.at[el])
-        arrived(out_dq.at[:, :, el], odq_r.at[el])
-        for n, out in enumerate((out_dk, out_dv)):
+        for n in BOTH:
             sent(dks.at[el, n, pl.ds(0, 448), :], odk_s.at[el, n])
-            arrived(out.at[:, el], odk_r.at[el, n])
 
 
 def solution(mesh):
@@ -437,30 +508,27 @@
         G = k.shape[1]
         R = H // G
         half = T // 2
-        delta = jnp.sum(do.astype(f32) * o.astype(f32), axis=-1)
-        l_in, d_in = (t.T.reshape(G, R, T) for t in (lse, delta))
-        q_in, do_in = (t.reshape(2, half, G, R, D).transpose(2, 0, 3, 1, 4) for t in (q, do))
-        k_in, v_in = (t.reshape(2, half, G, D).transpose(2, 0, 1, 3) for t in (k, v))
+        l_in = lse.T.reshape(G, R, T)
         hbm = pl.BlockSpec(memory_space=pl.ANY)
         V, S = pltpu.VMEM, pltpu.SemaphoreType.DMA
         S2, W = 2 * G * T, G * half
-        dq_o, dk_o, dv_o = pl.pallas_call(
+        return pl.pallas_call(
             _kernel,
             in_specs=[hbm] * 6,
-            out_specs=[hbm] * 3,
-            out_shape=[jax.ShapeDtypeStruct((G, R, 2, half, D), bf16)] + [jax.ShapeDtypeStruct((G, 2, half, D), bf16)] * 2,
+            out_specs=[pl.BlockSpec(memory_space=pltpu.VMEM)] * 3,
+            out_shape=[V((T, H, D), bf16)] + [V((T, G, D), bf16)] * 2,
             scratch_shapes=[
+                *[V((T, H, D), bf16)] * 3, *[V((T, G, D), bf16)] * 2, *[V((T * H, D), f32)] * 2,
+                *[V((G, 2, R, half, D), bf16)] * 2, *[V((G, 2, half, D), bf16)] * 2, V((G, R, T), f32),
+                V((G, R, 2, half, D), bf16), *[V((G, 2, half, D), bf16)] * 2,
                 V((2, R, S2, D), bf16), V((2, G, 2, R, T), f32), V((S2, T), f32), V((G, 2, 2, W, D), bf16), V((R, S2, D), f32),
                 V((G, 2, 2, D, W), f32), V((4, 2, 2, D, W), f32), V((4, 2, 2, D, W), f32), V((2, D, W), f32), V((2, R, W, D), f32),
                 V((2, R, W, D), bf16), V((2, 2, W, D), bf16),
-                *[S((G,))] * 4, *[S((2, G))] * 10, *[S((2,))] * 9,
+                *[S((G,))] * 5, *[S((2, G))] * 10, *[S((2,))] * 10,
             ],
             compiler_params=pltpu.CompilerParams(collective_id=0, has_side_effects=True, vmem_limit_bytes=60 << 20),
             cost_estimate=pl.CostEstimate(flops=46 << 30, bytes_accessed=8 << 20, transcendentals=36 << 20),
             name="attn_bwd",
-        )(q_in, do_in, l_in, d_in, k_in, v_in)
-        grad_q = dq_o.reshape(H, T, D).transpose(1, 0, 2)
-        grad_k, grad_v = (t.reshape(G, T, D).transpose(1, 0, 2) for t in (dk_o, dv_o))
-        return grad_q, grad_k, grad_v
+        )(q, do, o, k, v, l_in)
 
     return jax.shard_map(local, mesh=mesh, in_specs=(row_spec,) * 5 + (stat_spec,), out_specs=(row_spec,) * 3, check_vma=False)

time: 143 us -> 133 us (0.930)
  the two profiles are of different devices: /device:TPU:1 before, /device:TPU:16 now
where the time goes in v3:
time: 133 us
  Pallas kernels  130 us (98%)
  local copies, waits for them, and re-layouts  2.38 us (2%)
    pallas_call x1, Pallas kernels, local(): pl.pallas_call(_kernel, in_specs=[hbm] * 6, out_specs=[pl.BlockSpec(memor...  130 us

profile of v3, /device:TPU:16, one launch (start us, length us, event | category | flops | bytes accessed | tf_op | source)
XLA Modules:
  0.0 133.0 jit_solution(2947877952427777639)
XLA Ops:
  0.6 129.9 %attn_bwd.1 = (bf16[128,32,128]{2,1,0:T(8,128)(2,1)S(1)}, bf16[128,8,128]{2,1,0:T(8,128)(2,1)S(1)}, bf16[128,8,128]{2,1,0:T(8,128)(2,1)S(1)}) custom-call(bf16[128,32,128]{2,1,0:T(8,128)(2,1)} %q.1, bf16[128,32,128]{2,1,0:T(8,128)(2,1)} %do.1, bf16[128,32,128]{2,1,0:T(8,128)(2,1)} %o.1, bf16[128,8,128]{2,1,0:T(8,128)(2,1)} %k.1, bf16[128,8,128]{2,1,0:T(8,128)(2,1)} %v.1, ...), custom_call_target="tpu_custom_call" | custom-call | flops 49392123904 | bytes 8388608 | tf_op jit(solution)/shard_map/attn_bwd/pallas_call | solution.py:515
  130.6 1.0 copy.12
  131.6 0.7 copy.13
  132.3 0.7 copy.14

commit v4 on v3

--- a/solution.py
+++ b/solution.py
@@ -14,7 +14,7 @@
 MESH = pl.DeviceIdType.MESH
 BOTH, NEAR, AROUND = (0, 1), (1, 3), (1, 3, 2)
 STEPS = (("c1", "s1", "s3", "c3", "c2", "c0", "s2"), ("c1", "c3", "s1", "c2", "s3", "c0", "s2"), ("c1", "c3", "s1", "c2", "s2", "c0", "s3"))
-PASS = ("00s3E9", "00s3L5+", "00s1E4", "00s1L3+", "00s2E12", "00s2L14",
+PASS = ("00s3E9", "00s3L5+", "00s1E4", "00s1L3+", "00s2E12", "00s2L14v",
         "12s1E4", "33s1E5", "11s1L5+", "22s1L6", "11s3E9", "11s2E12", "11s2L13", "23s2E10", "23s3E13")
 
 def _pick(k, values):
@@ -26,9 +26,9 @@
 
 def _kernel(q, do, o, k, v, l_in, out_dq, out_dk, out_dv,
             qn, don, on, kn, vn, wide_q, wide_o, q_in, do_in, k_in, v_in, d_in, dqr, dkr, dvr,
-            qd, stb, st2, kv, dq, acc, rxy, rxz, rzf, dqx, dqs, dks, nat_s,
-            in_s, ql_r, fl_s, fl_r, kvg_s, kvg_r, ry_s, ry_r, rz_s, rz_r, odk_s, odk_r, dqx_s, dqx_r,
-            loc_s, kvo_r, st_r, qe_r, fe_s, fe_r, zf_s, zf_r, odq_s, odq_r):
+            qd, stb, st2, kv, dq, acc, rxy, rxz, rzf, dqx, dqs, dks,
+            nat_s, in_s, ql_r, fl_s, fl_r, zf_s, zf_r, kvg_s, kvg_r, ry_s, ry_r, rz_s, rz_r, odk_s, odk_r, dqx_s, dqx_r,
+            loc_s, kvo_r, st_r, qe_r, fe_s, fe_r, odq_s, odq_r):
     cy, cx = lax.axis_index("cy"), lax.axis_index("cx")
     T = q.shape[0]
     rem, div = lax.rem, lax.div
@@ -291,17 +291,19 @@
     for hh in (2, 3):
         partner_heads_in(hh)
 
-    def acc_y(k, d, kel):
-        return remote(acc.at[k + 1, kel], rxy.at[d, kel], ry_s.at[kel, d], ry_r.at[kel, d], across)
-
-    def acc_z(k, d, kel):
-        return remote(acc.at[k + 1, kel], rxz.at[z, kel], rz_s.at[kel, d], rz_r.at[kel, z], peer(2 * rem(z + d, 4) + bs))
-
-    def acc_f(k, d):
-        return remote(acc.at[k + 1, 1], rzf, zf_s.at[rem(d, 2) * div(d, 2)], zf_r.at[0], peer(2 * rem(z + d, 4) + bs))
-
-    def by_z_first(d):
-        return ((z == 0) & (rem(d, 2) == 1)) | ((z == 1) & (d == 1))
+    def acc_y(k, d, kel, m):
+        return remote(acc.at[k + 1, kel, m], rxy.at[d, kel, m], ry_s.at[kel, 2 * d + m], ry_r.at[kel, 2 * d + m], across)
+
+    def acc_z(k, d, kel, m):
+        to = peer(2 * rem(z + d, 4) + bs)
+        return remote(acc.at[k + 1, kel, m], rxz.at[z, kel, m], rz_s.at[kel, 2 * d + m], rz_r.at[kel, 2 * z + m], to)
+
+    def acc_f(k, d, m):
+        slot = jnp.where(d == 2, 2, m)
+        return remote(acc.at[k + 1, 1, m], rzf.at[slot], zf_s.at[2 * d + m], zf_r.at[slot], peer(2 * rem(z + d, 4) + bs))
+
+    def by_z_first(d, m):
+        return ((z == 0) & ((rem(d, 2) == 1) | ((d == 2) & (m == 1)))) | ((z == 1) & (d == 1))
 
     def step_of(k):
         d, cross = (_pick(z, [_pick(k, [of(name) for name in order]) for order in (*STEPS, STEPS[2])])
@@ -315,28 +317,29 @@
             k = STEPS[min(z_lo, 2)].index(entry[2:4])
 
             def go_on():
-                if not entry.endswith("+"):
-                    arrived(rxy.at[d, kel], ry_r.at[kel, d])
-                    acc[k + 1, kel] += rxy[d, kel]
-                acc_z(k, d, kel).start()
-
-            pl.when((n == int(entry[5:].rstrip("+"))) & (z >= z_lo) & (z <= z_hi))(go_on)
+                for m in BOTH:
+                    if not (entry.endswith("+") or entry.endswith("v" * m or "-")):
+                        arrived(rxy.at[d, kel, m], ry_r.at[kel, 2 * d + m])
+                        acc[k + 1, kel, m] += rxy[d, kel, m]
+                    acc_z(k, d, kel, m).start()
+
+            pl.when((n == int(entry[5:].rstrip("+v"))) & (z >= z_lo) & (z <= z_hi))(go_on)
 
     def late_across(k, d):
-        zfirst = by_z_first(d)
-
-        @pl.when(zfirst)
-        def _():
-            acc_f(k, d).start()
+        def add_in(m, slot):
+            arrived(rzf.at[slot], zf_r.at[slot])
+            acc[k + 1, 1, m] += rzf[slot]
 
         @pl.when((d == 0) & (z > 0))
         def _():
-            arrived(rzf, zf_r.at[0])
-            acc[k + 1, 1] += rzf[...]
-
-        @pl.when(jnp.logical_not(zfirst))
-        def _():
-            acc_y(k, d, 1).start()
+            for m in BOTH:
+                add_in(m, m)
+            pl.when(z == 2)(lambda: add_in(1, 2))
+
+        for m in BOTH:
+            zfirst = by_z_first(d, m)
+            pl.when(zfirst)(lambda: acc_f(k, d, m).start())
+            pl.when(jnp.logical_not(zfirst))(lambda: acc_y(k, d, 1, m).start())
 
     def heads(p):
         return pl.ds(2 * p, 2)
@@ -353,20 +356,19 @@
         dqr[h, heads(p), el] = dqs[el, heads(p), block(el, i), :]
 
     def full_unit(n, carry):
-        k, sub = div(n, 2), rem(n, 2)
+        at = jnp.where((z == 3) & (n > 0) & (n < 3), 3 - n, n)
+        k, sub = div(at, 2), rem(at, 2)
         d, cross, g, gt = step_of(k)
         el = 1 - sub + sub * gt
         kel = sub * gt
 
-        last = div(z, 3)
-
-        @pl.when(n == 2 - last)
-        def _():
-            pl.when(z == 3)(lambda: late_heads(1 - c))
+        @pl.when(n == 2)
+        def _():
             arrived(qd.at[:, :, seven], qe_r.at[0])
             fw_early().start()
-
-        @pl.when(n == 3 - 2 * last)
+            pl.when(z == 3)(lambda: late_heads(1 - c))
+
+        @pl.when(n == 3 - div(z, 3))
         def _():
             arrived(qd.at[:, :, half(1 - c, 0), :], fe_r.at[0])
 
@@ -387,7 +389,8 @@
 
         @pl.when((cross == 1) & (sub == 1 - gt))
         def _():
-            acc_y(k, d, 0).start()
+            for m in BOTH:
+                acc_y(k, d, 0, m).start()
 
         pass_at(n)
 
@@ -430,26 +433,26 @@
         finish_dq(1, 1)
 
 
-    def take(ref, rsem, el):
-        arrived(ref, rsem)
-        acc[0, el] += ref[...]
-
-    for el in BOTH:
-        for d in AROUND:
-            zs = rem(z + d, 4)
-
-            def take_z():
-                take(rxz.at[zs, el], rz_r.at[el, zs], el)
-
-            take_z() if el == 0 else pl.when(z > zs)(take_z)
-
-        def take_y():
-            take(rxy.at[0, el], ry_r.at[el, 0], el)
-
-        take_y() if el == 0 else pl.when((bs == 1) | (z > 0))(take_y)
-        dks[el, 0] = (jnp.transpose(acc[0, el, 0]) * SCALE).astype(bf16)
-        dks[el, 1] = jnp.transpose(acc[0, el, 1]).astype(bf16)
+    for el in BOTH:
         for n, got in enumerate((dkr, dvr)):
+            def take(ref, rsem):
+                arrived(ref, rsem)
+                acc[0, el, n] += ref[...]
+
+            for d in AROUND:
+                zs = rem(z + d, 4)
+
+                def take_z():
+                    take(rxz.at[zs, el, n], rz_r.at[el, 2 * zs + n])
+
+                take_z() if el == 0 else pl.when(z > zs)(take_z)
+
+            def take_y():
+                take(rxy.at[0, el, n], ry_r.at[el, n])
+
+            take_y() if el == 0 else pl.when((bs == 1) | (z > 0))(take_y)
+            total = jnp.transpose(acc[0, el, n])
+            dks[el, n] = (total * SCALE if n == 0 else total).astype(bf16)
             for t, (dev, _) in enumerate(others):
                 remote(dks.at[el, n, block(el, rem(i + t + 1, 8)), :], got.at[h, el], odk_s.at[el, n], odk_r.at[el, n], dev).start()
             got[h, el] = dks[el, n, block(el, i), :]
@@ -481,22 +484,21 @@
     for k, name in enumerate(STEPS[0]):
         d, cross = int(name[1]), int(name[0] == "c")
         made = acc_y if cross else acc_z
-        made(k, d, 0).wait_send()
         later = 2 * rem(z + d, 4) + rem(bs + cross, 2) > s
-        if not cross:
-            pl.when(later)(lambda: made(k, d, 1).wait_send())
-        elif d == 0:
-            pl.when(later | (z > 0))(lambda: made(k, d, 1).wait_send())
-        else:
-            zfirst = by_z_first(d)
-            pl.when(zfirst)(lambda: acc_f(k, d).wait_send())
-            pl.when(later & jnp.logical_not(zfirst))(lambda: made(k, d, 1).wait_send())
+        if name == "c0":
+            later = later | (z > 0)
+        for m in BOTH:
+            made(k, d, 0, m).wait_send()
+            zfirst = by_z_first(d, m) if cross and d > 0 else later & False
+            pl.when(later & jnp.logical_not(zfirst))(lambda: made(k, d, 1, m).wait_send())
+            if cross and d > 0:
+                pl.when(zfirst)(lambda: acc_f(k, d, m).wait_send())
     for el in BOTH:
         for p in BOTH:
             dqx_copy(el, p).wait_send()
-        sent(dqs.at[el, :, pl.ds(0, 448), :], odq_s.at[el])
+        sent(dqs.at[el, :, seven, :], odq_s.at[el])
         for n in BOTH:
-            sent(dks.at[el, n, pl.ds(0, 448), :], odk_s.at[el, n])
+            sent(dks.at[el, n, seven, :], odk_s.at[el, n])
 
 
 def solution(mesh):
@@ -522,9 +524,9 @@
                 *[V((G, 2, R, half, D), bf16)] * 2, *[V((G, 2, half, D), bf16)] * 2, V((G, R, T), f32),
                 V((G, R, 2, half, D), bf16), *[V((G, 2, half, D), bf16)] * 2,
                 V((2, R, S2, D), bf16), V((2, G, 2, R, T), f32), V((S2, T), f32), V((G, 2, 2, W, D), bf16), V((R, S2, D), f32),
-                V((G, 2, 2, D, W), f32), V((4, 2, 2, D, W), f32), V((4, 2, 2, D, W), f32), V((2, D, W), f32), V((2, R, W, D), f32),
+                V((G, 2, 2, D, W), f32), *[V((4, 2, 2, D, W), f32)] * 2, V((3, D, W), f32), V((2, R, W, D), f32),
                 V((2, R, W, D), bf16), V((2, 2, W, D), bf16),
-                *[S((G,))] * 5, *[S((2, G))] * 10, *[S((2,))] * 10,
+                *[S((G,))] * 7, *[S((2, G))] * 10, *[S((2,))] * 8,
             ],
             compiler_params=pltpu.CompilerParams(collective_id=0, has_side_effects=True, vmem_limit_bytes=60 << 20),
             cost_estimate=pl.CostEstimate(flops=46 << 30, bytes_accessed=8 << 20, transcendentals=36 << 20),

time: 133 us -> 129 us (0.970)
  the two profiles are of different devices: /device:TPU:16 before, /device:TPU:1 now
where the time goes in v4:
time: 129 us
  Pallas kernels  126 us (98%)
  local copies, waits for them, and re-layouts  2.38 us (2%)
    pallas_call x1, Pallas kernels, local(): pl.pallas_call(_kernel, in_specs=[hbm] * 6, out_specs=[pl.BlockSpec(memor...  126 us

profile of v4, /device:TPU:1, one launch (start us, length us, event | category | flops | bytes accessed | tf_op | source)
XLA Modules:
  0.0 129.2 jit_solution(10422732872383879232)
XLA Ops:
  0.6 126.2 %attn_bwd.1 = (bf16[128,32,128]{2,1,0:T(8,128)(2,1)S(1)}, bf16[128,8,128]{2,1,0:T(8,128)(2,1)S(1)}, bf16[128,8,128]{2,1,0:T(8,128)(2,1)S(1)}) custom-call(bf16[128,32,128]{2,1,0:T(8,128)(2,1)} %q.1, bf16[128,32,128]{2,1,0:T(8,128)(2,1)} %do.1, bf16[128,32,128]{2,1,0:T(8,128)(2,1)} %o.1, bf16[128,8,128]{2,1,0:T(8,128)(2,1)} %k.1, bf16[128,8,128]{2,1,0:T(8,128)(2,1)} %v.1, ...), custom_call_target="tpu_custom_call" | custom-call | flops 49392123904 | bytes 8388608 | tf_op jit(solution)/shard_map/attn_bwd/pallas_call | solution.py:517
  126.8 1.0 copy.12
  127.8 0.7 copy.13
  128.5 0.7 copy.14

commit v5 on v4

--- a/solution.py
+++ b/solution.py
@@ -24,7 +24,7 @@
     return r
 
 
-def _kernel(q, do, o, k, v, l_in, out_dq, out_dk, out_dv,
+def _kernel(q, do, o, k, v, l_in, out_dq, out_dkv,
             qn, don, on, kn, vn, wide_q, wide_o, q_in, do_in, k_in, v_in, d_in, dqr, dkr, dvr,
             qd, stb, st2, kv, dq, acc, rxy, rxz, rzf, dqx, dqs, dks,
             nat_s, in_s, ql_r, fl_s, fl_r, zf_s, zf_r, kvg_s, kvg_r, ry_s, ry_r, rz_s, rz_r, odk_s, odk_r, dqx_s, dqx_r,
@@ -50,7 +50,7 @@
     across = peer(pair)
     partner = {"cy": cy, "cx": cx + 1 - 2 * c}
     others = [member(rem(i + t, 8)) for t in range(1, 8)]
-    seven = pl.ds(0, 7 * 64)
+    others_, seven = pl.ds(0, 7), pl.ds(0, 7 * 64)
 
     def block(el, i2):
         return pl.ds(pl.multiple_of((i2 + el * (7 - 2 * i2)) * 64, 64), 64)
@@ -181,7 +181,7 @@
                     st2[rows(cp, el, i2), 4 * n:4 * n + 4] = tile[64 * el:64 * el + 64]
 
     st_fw = remote(stb.at[c], stb.at[c], fe_s.at[1], fe_r.at[1], partner)
-    arrived(stb.at[c, pl.ds(0, 7)], st_r.at[0])
+    arrived(stb.at[c, others_], st_r.at[0])
     pltpu.make_async_copy(l_in.at[h], stb.at[c, i, 0], loc_s.at[0]).wait()
     st_fw.start()
     build_stats(c)
@@ -264,6 +264,10 @@
             arrived(kv.at[pair, 0], kvg_r.at[0, pair])
             spread_all(pair, 0, 3, NEAR, start)
 
+        @pl.when(m == 2)
+        def _():
+            send_early()
+
         @pl.when(m == 3)
         def _():
             arrived(kv.at[pair, 1], kvg_r.at[1, pair])
@@ -283,7 +287,6 @@
     def late_heads(cp):
         lax.fori_loop(2, 4, lambda hh, carry: own_tiles(hh, cp), None)
 
-    send_early()
     lax.fori_loop(0, 4, own_unit, 0)
     for hh in (2, 3):
         heads_in(hh)
@@ -457,22 +460,22 @@
                 remote(dks.at[el, n, block(el, rem(i + t + 1, 8)), :], got.at[h, el], odk_s.at[el, n], odk_r.at[el, n], dev).start()
             got[h, el] = dks[el, n, block(el, i), :]
 
-    def by_token(got, el, heads_, wide, out):
+    def by_token(got, el, heads_, wide, out, first=0):
         for j in range(heads_):
             wide[pl.ds(j + 64 * el * heads_, 64, stride=heads_), :] = got(j).astype(f32)
         for t in range(64 * el, 64 * el + 64, 16):
-            out[pl.ds(t, 16)] = wide[pl.ds(t * heads_, 16 * heads_), :].reshape(16, heads_, out.shape[2]).astype(bf16)
-
-    for el in BOTH:
-        arrived(dqr.at[pl.ds(0, 7), :, el], odq_r.at[el])
+            out[pl.ds(t, 16), first:first + heads_] = wide[pl.ds(t * heads_, 16 * heads_), :].reshape(16, heads_, out.shape[2]).astype(bf16)
+
+    for el in BOTH:
+        arrived(dqr.at[others_, :, el], odq_r.at[el])
         by_token(lambda j: dqr[j // 4, j % 4, el], el, 32, wide_q, out_dq)
     for el in BOTH:
-        for n, (got, out) in enumerate(((dkr, out_dk), (dvr, out_dv))):
-            arrived(got.at[pl.ds(0, 7), el], odk_r.at[el, n])
-            by_token(lambda j: got[j, el], el, 8, wide_o, out)
+        for n, got in enumerate((dkr, dvr)):
+            arrived(got.at[others_, el], odk_r.at[el, n])
+            by_token(lambda j: got[j, el], el, 8, wide_o, out_dkv, 8 * n)
 
     for n, src in enumerate((k_in, v_in, q_in, do_in, l_in, d_in)):
-        sent(src.at[pl.ds(0, 7)], in_s.at[n])
+        sent(src.at[others_], in_s.at[n])
     for el in BOTH:
         to_across(el).wait_send()
         spread_all(s, el, 0, AROUND, lambda cp: cp.wait_send())
@@ -514,11 +517,11 @@
         hbm = pl.BlockSpec(memory_space=pl.ANY)
         V, S = pltpu.VMEM, pltpu.SemaphoreType.DMA
         S2, W = 2 * G * T, G * half
-        return pl.pallas_call(
+        grad_q, grad_kv = pl.pallas_call(
             _kernel,
             in_specs=[hbm] * 6,
-            out_specs=[pl.BlockSpec(memory_space=pltpu.VMEM)] * 3,
-            out_shape=[V((T, H, D), bf16)] + [V((T, G, D), bf16)] * 2,
+            out_specs=[pl.BlockSpec(memory_space=pltpu.VMEM)] * 2,
+            out_shape=[V((T, H, D), bf16), V((T, 2 * G, D), bf16)],
             scratch_shapes=[
                 *[V((T, H, D), bf16)] * 3, *[V((T, G, D), bf16)] * 2, *[V((T * H, D), f32)] * 2,
                 *[V((G, 2, R, half, D), bf16)] * 2, *[V((G, 2, half, D), bf16)] * 2, V((G, R, T), f32),
@@ -532,5 +535,6 @@
             cost_estimate=pl.CostEstimate(flops=46 << 30, bytes_accessed=8 << 20, transcendentals=36 << 20),
             name="attn_bwd",
         )(q, do, o, k, v, l_in)
+        return grad_q, grad_kv[:, :G], grad_kv[:, G:]
 
     return jax.shard_map(local, mesh=mesh, in_specs=(row_spec,) * 5 + (stat_spec,), out_specs=(row_spec,) * 3, check_vma=False)

time: 129 us -> 129 us (level)
    unnamed x3 -> x1, local copies, waits for them, and re-layouts: 2.38 us -> 0.97 us
where the time goes in v5:
time: 129 us; the launch traced here: 128 us
  Pallas kernels  126 us (98%)
  local copies, waits for them, and re-layouts  1.8 us (1%)
    pallas_call x1, Pallas kernels, local(): pl.pallas_call(_kernel, in_specs=[hbm] * 6, out_specs=[pl.BlockSpec(memor...  126 us

profile of v5, /device:TPU:1, one launch (start us, length us, event | category | flops | bytes accessed | tf_op | source)
XLA Modules:
  0.0 128.5 jit_solution(11105038814100313269)
XLA Ops:
  0.6 126.1 %attn_bwd.1 = (bf16[128,32,128]{2,1,0:T(8,128)(2,1)S(1)}, bf16[128,16,128]{2,1,0:T(8,128)(2,1)S(1)}) custom-call(bf16[128,32,128]{2,1,0:T(8,128)(2,1)} %q.1, bf16[128,32,128]{2,1,0:T(8,128)(2,1)} %do.1, bf16[128,32,128]{2,1,0:T(8,128)(2,1)} %o.1, bf16[128,8,128]{2,1,0:T(8,128)(2,1)} %k.1, bf16[128,8,128]{2,1,0:T(8,128)(2,1)} %v.1, f32[8,4,128]{2,1,0:T(4,128)} %bitcast.3), custom_call_target="tpu_custom_call" | custom-call | flops 49392123904 | bytes 8388608 | tf_op jit(solution)/shard_map/attn_bwd/pallas_call | solution.py:520
  126.7 1.0 copy.10
  127.7 0.8 fusion

commit v6 on v5

--- a/solution.py
+++ b/solution.py
@@ -14,7 +14,7 @@
 MESH = pl.DeviceIdType.MESH
 BOTH, NEAR, AROUND = (0, 1), (1, 3), (1, 3, 2)
 STEPS = (("c1", "s1", "s3", "c3", "c2", "c0", "s2"), ("c1", "c3", "s1", "c2", "s3", "c0", "s2"), ("c1", "c3", "s1", "c2", "s2", "c0", "s3"))
-PASS = ("00s3E9", "00s3L5+", "00s1E4", "00s1L3+", "00s2E12", "00s2L14v",
+PASS = ("00s3E9", "00s3L5+", "00s1E4", "00s1L3+", "00s2E12", "00s2L13v",
         "12s1E4", "33s1E5", "11s1L5+", "22s1L6", "11s3E9", "11s2E12", "11s2L13", "23s2E10", "23s3E13")
 
 def _pick(k, values):

time: 129 us -> 129 us (level)
  no operation moved by 1% of the time
where the time goes in v6:
time: 129 us; the launch traced here: 128 us
  Pallas kernels  126 us (98%)
  local copies, waits for them, and re-layouts  1.8 us (1%)
    pallas_call x1, Pallas kernels, local(): pl.pallas_call(_kernel, in_specs=[hbm] * 6, out_specs=[pl.BlockSpec(memor...  126 us

profile of v6, /device:TPU:1, one launch (start us, length us, event | category | flops | bytes accessed | tf_op | source)
XLA Modules:
  0.0 128.0 jit_solution(14542711070122194744)
XLA Ops:
  0.6 125.6 %attn_bwd.1 = (bf16[128,32,128]{2,1,0:T(8,128)(2,1)S(1)}, bf16[128,16,128]{2,1,0:T(8,128)(2,1)S(1)}) custom-call(bf16[128,32,128]{2,1,0:T(8,128)(2,1)} %q.1, bf16[128,32,128]{2,1,0:T(8,128)(2,1)} %do.1, bf16[128,32,128]{2,1,0:T(8,128)(2,1)} %o.1, bf16[128,8,128]{2,1,0:T(8,128)(2,1)} %k.1, bf16[128,8,128]{2,1,0:T(8,128)(2,1)} %v.1, f32[8,4,128]{2,1,0:T(4,128)} %bitcast.3), custom_call_target="tpu_custom_call" | custom-call | flops 49392123904 | bytes 8388608 | tf_op jit(solution)/shard_map/attn_bwd/pallas_call | solution.py:520
  126.2 1.0 copy.10
  127.2 0.8 fusion
